TPU v7x, 128 devices: a 2x2x16 block of a 8x8x16 slice. The times are simulated.
128 devices in a mesh: groups: 4 (over y, x), gx: 16 (over z), gy: 2 (over core).
Axes of the slice: x: 2, y: 2, z: 16, core: 2. Of those that a mesh axis runs over, the one named last changes fastest.
The devices are a block of a 8x8x16 slice.
Arguments:
- source: float32 [4, 3, 2, 64, 64, 256], P('groups', None, None, 'gx', 'gy'), parts along dimension 0, may hold values from -12 to 12
- permittivity: float32 [12, 64, 64, 256], P('groups', 'gx', 'gy'), parts along dimension 0, may hold values from 1 to 12
- frequency: float32 [1], replicated, may hold values from 0.25 to 0.6
Outputs:
- solution: float32 [4, 3, 2, 64, 64, 256], P('groups', None, None, 'gx', 'gy'), parts along dimension 0
- residual: float32 [4, 3, 2, 64, 64, 256], P('groups', None, None, 'gx', 'gy'), parts along dimension 0
There are 4 independent parts, one for each index of `groups`. A program takes and returns all parts, laid end to end along the dimension named above; an argument that names none is the same for every part. Nothing has to cross between parts.
All inputs are finite; a program needn't handle non-finite values.
Results may differ from a plain program's by a relative error of at most 0.0003.
Values sent between devices are 32-bit elements; how exact they have to be, the bound alone decides.
No kernel may reach another device: no remote copies, remote signals or barrier semaphores. Data moves between devices by JAX's collectives and lax.ppermute only.
A program may use at most 64 MiB of HBM per device.

v0:
```python
import jax
import jax.numpy as jnp
from jax import lax
from jax.sharding import PartitionSpec as P

NZ = 256
PML = 8
ITERS = 3


pml_strength = 2.0


def with_halo(block, sides, width):
    for axis, dim in sides:
        count = lax.axis_size(axis)
        forward = [(i, i + 1) for i in range(count - 1)]
        backward = [(target, source) for source, target in forward]
        low = lax.ppermute(
            lax.slice_in_dim(block, block.shape[dim] - width, None, axis=dim), axis, forward
        )
        high = lax.ppermute(lax.slice_in_dim(block, 0, width, axis=dim), axis, backward)
        block = jnp.concatenate([low, block, high], axis=dim)
    return block


def sent_to_all(array, axis):
    copies = jnp.broadcast_to(array, (lax.axis_size(axis), *array.shape))
    return lax.all_to_all(copies, axis, split_axis=0, concat_axis=0, tiled=True)


def over_copies(array, axis):
    everything = sent_to_all(array, axis)
    return jnp.sum(everything, axis=0)


def in_one(arrays, axis):
    line, at, finished = (jnp.concatenate([a.reshape(-1) for a in arrays]), 0, [])
    running = over_copies(line, axis)
    for a in arrays:
        finished.append(running[at : at + a.size].reshape(a.shape))
        at += a.size
    return tuple(finished)


def stretch(points, length, frequency):
    inside = jnp.maximum(jnp.maximum(PML - points, points - (length - PML)), 0.0) / PML
    damping = pml_strength * inside**3 / frequency[:, None]
    factor = 1.0 / (1.0 + damping * damping)
    return jnp.stack([factor, -damping * factor], axis=1)


def orient(coefficient, dimension):
    target = [coefficient.shape[0], 2, 1, 1, 1]
    target[dimension] = coefficient.shape[2]
    return coefficient.reshape(target)


def times_coef(values, coefficient):
    real_part = values[:, 0] * coefficient[:, 0] - values[:, 1] * coefficient[:, 1]
    imag_part = values[:, 0] * coefficient[:, 1] + values[:, 1] * coefficient[:, 0]
    return jnp.stack([real_part, imag_part], axis=1)


def curl_forward(extended, front_x, front_y, front_z):
    centre = extended[:, :, :, :-1, :-1]

    def step_x(component):
        return extended[:, component, :, 1:, :-1] - centre[:, component]

    def step_y(component):
        return extended[:, component, :, :-1, 1:] - centre[:, component]

    def step_z(component):
        cells = centre[:, component]
        above = jnp.concatenate([cells[..., 1:], jnp.zeros_like(cells[..., :1])], axis=-1)
        return above - cells

    curl_x = times_coef(step_y(2), front_y) - times_coef(step_z(1), front_z)
    curl_y = times_coef(step_z(0), front_z) - times_coef(step_x(2), front_x)
    curl_z = times_coef(step_x(1), front_x) - times_coef(step_y(0), front_y)
    return jnp.stack([curl_x, curl_y, curl_z], axis=1)


def curl_backward(padded, back_x, back_y, back_z):
    centre = padded[:, :, :, 1:, 1:]

    def step_x(component):
        return centre[:, component] - padded[:, component, :, :-1, 1:]

    def step_y(component):
        return centre[:, component] - padded[:, component, :, 1:, :-1]

    def step_z(component):
        cells = centre[:, component]
        below = jnp.concatenate([jnp.zeros_like(cells[..., :1]), cells[..., :-1]], axis=-1)
        return cells - below

    out_x = times_coef(step_y(2), back_y) - times_coef(step_z(1), back_z)
    out_y = times_coef(step_z(0), back_z) - times_coef(step_x(2), back_x)
    out_z = times_coef(step_x(1), back_x) - times_coef(step_y(0), back_y)
    return jnp.stack([out_x, out_y, out_z], axis=1)


def scaled(values, number):
    real_scale = number[0].reshape(-1, 1, 1, 1, 1)
    imag_scale = number[1].reshape(-1, 1, 1, 1, 1)
    real_part = values[:, :, 0] * real_scale - values[:, :, 1] * imag_scale
    imag_part = values[:, :, 0] * imag_scale + values[:, :, 1] * real_scale
    return jnp.stack([real_part, imag_part], axis=2)


def product(left, right):
    real_part = jnp.sum(
        left[:, :, 0] * right[:, :, 0] + left[:, :, 1] * right[:, :, 1], axis=(1, 2, 3, 4)
    )
    imag_part = jnp.sum(
        left[:, :, 0] * right[:, :, 1] - left[:, :, 1] * right[:, :, 0], axis=(1, 2, 3, 4)
    )
    return jnp.stack([real_part, imag_part])


def complex_times(first, other):
    return jnp.stack(
        [first[0] * other[0] - first[1] * other[1], first[0] * other[1] + first[1] * other[0]]
    )


def complex_ratio(first, other):
    modulus = other[0] * other[0] + other[1] * other[1]
    return (
        jnp.stack(
            [first[0] * other[0] + first[1] * other[1], first[1] * other[0] - first[0] * other[1]]
        )
        / modulus
    )


def grid_points(start, first, count):
    return (start + jnp.arange(first, count, dtype=jnp.int32)).astype(jnp.float32)


def body(source, permittivity, frequency):
    cells_x = source.shape[3]
    cells_y = source.shape[4]
    total_x = cells_x * lax.axis_size("gx")
    total_y = cells_y * lax.axis_size("gy")
    index_x = lax.axis_index("gx")
    index_y = lax.axis_index("gy")
    margin = 1
    front_x = orient(
        stretch(grid_points(index_x * cells_x, -margin, cells_x) + 0.5, total_x, frequency), 2
    )
    front_y = orient(
        stretch(grid_points(index_y * cells_y, -margin, cells_y) + 0.5, total_y, frequency), 3
    )
    back_x = orient(stretch(grid_points(index_x * cells_x, 0, cells_x), total_x, frequency), 2)
    back_y = orient(stretch(grid_points(index_y * cells_y, 0, cells_y), total_y, frequency), 3)
    z_points = grid_points(0, 0, NZ)
    front_z = orient(stretch(z_points + 0.5, NZ, frequency), 4)
    back_z = orient(stretch(z_points, NZ, frequency), 4)
    material = (frequency * frequency).reshape(-1, 1, 1, 1, 1, 1) * permittivity[None, :, None]

    def operate(values):
        extended = with_halo(values, (("gx", 3), ("gy", 4)), 1)
        keep_x = jnp.where((jnp.arange(cells_x + 1) > 0) | (index_x > 0), 1.0, 0.0).astype(
            jnp.float32
        )
        keep_y = jnp.where((jnp.arange(cells_y + 1) > 0) | (index_y > 0), 1.0, 0.0).astype(
            jnp.float32
        )
        rotated = curl_forward(extended, front_x, front_y, front_z)
        padded = rotated * keep_x.reshape(1, 1, 1, -1, 1, 1) * keep_y.reshape(1, 1, 1, 1, -1, 1)
        applied = curl_backward(padded, back_x, back_y, back_z)
        return applied - material * values

    solution = jnp.zeros_like(source)
    residual = source
    direction = source
    shadow_dot = over_copies(product(source, residual), ("gx", "gy"))
    for iteration in range(ITERS):
        applied = operate(direction)
        step_size = complex_ratio(shadow_dot, over_copies(product(source, applied), ("gx", "gy")))
        middle = residual - scaled(applied, step_size)
        second = operate(middle)
        sums_triple = in_one(
            (product(second, middle), product(second, second), product(source, second)),
            ("gx", "gy"),
        )
        weight = complex_ratio(sums_triple[0], sums_triple[1])
        solution = solution + scaled(direction, step_size) + scaled(middle, weight)
        residual = middle - scaled(second, weight)
        if iteration + 1 < ITERS:
            shadow_next = -complex_times(weight, sums_triple[2])
            momentum = complex_times(
                complex_ratio(shadow_next, shadow_dot), complex_ratio(step_size, weight)
            )
            direction = residual + scaled(direction - scaled(applied, weight), momentum)
            shadow_dot = shadow_next
    return (solution, residual)


def solution(mesh):
    placed = (P("groups", None, None, "gx", "gy", None), P("groups", "gx", "gy", None), P())
    return jax.shard_map(
        body,
        mesh=mesh,
        in_specs=placed,
        out_specs=(
            P("groups", None, None, "gx", "gy", None),
            P("groups", None, None, "gx", "gy", None),
        ),
        check_vma=False,
    )
```

profile of v0, /device:TPU:69, one launch (start us, length us, event | category | flops | bytes accessed | tf_op | source)
XLA Modules:
  0.0 425.0 jit_solution(13874893840532838654)
XLA Ops:
  3.1 5.2 %collective-permute-start = (f32[1,3,2,1,32,256]{5,4,3,2,1,0:T(8,128)S(1)}, f32[1,3,2,1,32,256]{5,4,3,2,1,0:T(8,128)S(1)}, u32[]{:S(2)}, u32[]{:S(2)}) collective-permute-start(f32[1,3,2,1,32,256]{5,4,3,2,1,0:T(8,128)S(1)} %get-tuple-element.185), channel_id=1, source_target_pairs={{0,2},{2,4},{4,6},{6,8},{8,10},{10,12},{12,14},{14,16},{16,18},{18... | collective-permute-start | bytes 589832 | tf_op jit(solution)/shard_map/ppermute | solution.py:19
  11.1 11.8 %collective-permute-start.2 = (f32[1,3,2,6,1,256]{5,4,3,2,1,0:T(1,128)S(1)}, f32[1,3,2,6,1,256]{5,4,3,2,1,0:T(1,128)S(1)}, u32[]{:S(2)}, u32[]{:S(2)}) collective-permute-start(f32[1,3,2,6,1,256]{5,4,3,2,1,0:T(1,128)S(1)} %get-tuple-element.134), channel_id=1, source_target_pairs={{1,0},{3,2},{5,4},{7,6},{9,8},{11,10},{13,12},{15,14},{17,16},{19,... | collective-permute-start | bytes 110600 | tf_op jit(solution)/shard_map/ppermute | solution.py:22
  31.6 11.5 %all-to-all-start = ((f32[32,2,1]{1,2,0:T(1,128)}), f32[32,2,1]{1,2,0:T(1,128)S(1)}, u32[]{:S(2)}, u32[]{:S(2)}) async-start(f32[32,2,1]{1,2,0:T(1,128)} %broadcast_in_dim.76), calls=%async_computation | async-start | bytes 32768 | tf_op jit(solution)/shard_map/all_to_all | solution.py:29
  44.4 10.2 %all-to-all-done = f32[32,2,1]{1,2,0:T(1,128)S(1)} async-done(((f32[32,2,1]{1,2,0:T(1,128)}), f32[32,2,1]{1,2,0:T(1,128)S(1)}, u32[]{:S(2)}, u32[]{:S(2)}) %all-to-all-start) | async-done | bytes 288 | tf_op jit(solution)/shard_map/all_to_all | solution.py:29
  55.2 4.7 %all-to-all-start.1 = ((f32[32,2,1]{1,2,0:T(1,128)}), f32[32,2,1]{1,2,0:T(1,128)S(1)}, u32[]{:S(2)}, u32[]{:S(2)}) async-start(f32[32,2,1]{1,2,0:T(1,128)} %broadcast_in_dim.79), calls=%async_computation.1 | async-start | bytes 32768 | tf_op jit(solution)/shard_map/all_to_all | solution.py:29
  60.6 11.1 %all-to-all-done.1 = f32[32,2,1]{1,2,0:T(1,128)S(1)} async-done(((f32[32,2,1]{1,2,0:T(1,128)}), f32[32,2,1]{1,2,0:T(1,128)S(1)}, u32[]{:S(2)}, u32[]{:S(2)}) %all-to-all-start.1) | async-done | bytes 288 | tf_op jit(solution)/shard_map/all_to_all | solution.py:29
  87.5 3.9 collective-permute-done.5
  92.7 4.1 collective-permute-start.6
  108.7 5.9 %all-to-all-start.2 = ((f32[32,1,6]{2,1,0:T(1,128)}), f32[32,1,6]{2,1,0:T(1,128)S(1)}, u32[]{:S(2)}, u32[]{:S(2)}) async-start(f32[32,1,6]{2,1,0:T(1,128)} %broadcast_in_dim.80), calls=%async_computation.2 | async-start | bytes 32768 | tf_op jit(solution)/shard_map/all_to_all | solution.py:29
  117.2 9.0 %all-to-all-done.2 = f32[32,1,6]{2,1,0:T(1,128)S(1)} async-done(((f32[32,1,6]{2,1,0:T(1,128)}), f32[32,1,6]{2,1,0:T(1,128)S(1)}, u32[]{:S(2)}, u32[]{:S(2)}) %all-to-all-start.2) | async-done | bytes 800 | tf_op jit(solution)/shard_map/all_to_all | solution.py:29
  170.5 3.9 collective-permute-done.9
  175.7 4.2 collective-permute-start.10
  188.5 17.5 %all_to_all.38 = f32[32,2,1]{1,2,0:T(1,128)S(1)} all-to-all(f32[32,2,1]{1,2,0:T(1,128)S(1)} %broadcast_in_dim.81), channel_id=1, replica_groups=mesh['groups'=4,'gx'=16,'gy'=2] {'gx','gy'}, dimensions={0} | all-to-all | bytes 512 | tf_op jit(solution)/shard_map/all_to_all | solution.py:29
  214.5 2.4 multiply_subtract_fusion.8
  222.8 3.9 collective-permute-done.13
  228.1 4.0 collective-permute-start.14
  244.2 6.1 %all-to-all-start.4 = ((f32[32,1,6]{2,1,0:T(1,128)}), f32[32,1,6]{2,1,0:T(1,128)S(1)}, u32[]{:S(2)}, u32[]{:S(2)}) async-start(f32[32,1,6]{2,1,0:T(1,128)} %broadcast_in_dim.82), calls=%async_computation.4 | async-start | bytes 32768 | tf_op jit(solution)/shard_map/all_to_all | solution.py:29
  252.8 9.1 %all-to-all-done.4 = f32[32,1,6]{2,1,0:T(1,128)S(1)} async-done(((f32[32,1,6]{2,1,0:T(1,128)}), f32[32,1,6]{2,1,0:T(1,128)S(1)}, u32[]{:S(2)}, u32[]{:S(2)}) %all-to-all-start.4) | async-done | bytes 800 | tf_op jit(solution)/shard_map/all_to_all | solution.py:29
  297.0 2.6 multiply_subtract_fusion.5
  308.6 3.9 collective-permute-done.17
  313.8 4.2 collective-permute-start.18
  328.2 6.1 %all-to-all-start.5 = ((f32[32,2,1]{1,2,0:T(1,128)}), f32[32,2,1]{1,2,0:T(1,128)S(1)}, u32[]{:S(2)}, u32[]{:S(2)}) async-start(f32[32,2,1]{1,2,0:T(1,128)} %broadcast_in_dim.83), calls=%async_computation.5 | async-start | bytes 32768 | tf_op jit(solution)/shard_map/all_to_all | solution.py:29
  336.6 9.3 %all-to-all-done.5 = f32[32,2,1]{1,2,0:T(1,128)S(1)} async-done(((f32[32,2,1]{1,2,0:T(1,128)}), f32[32,2,1]{1,2,0:T(1,128)S(1)}, u32[]{:S(2)}, u32[]{:S(2)}) %all-to-all-start.5) | async-done | bytes 288 | tf_op jit(solution)/shard_map/all_to_all | solution.py:29
  354.9 2.4 multiply_subtract_fusion.2
  363.9 3.6 collective-permute-done.21
  368.9 2.4 multiply_subtract_fusion.7
  371.2 4.0 collective-permute-start.22
  381.9 3.2 add_reduce_fusion.2
  389.5 6.1 %all-to-all-start.6 = ((f32[32,1,6]{2,1,0:T(1,128)}), f32[32,1,6]{2,1,0:T(1,128)S(1)}, u32[]{:S(2)}, u32[]{:S(2)}) async-start(f32[32,1,6]{2,1,0:T(1,128)} %broadcast_in_dim.84), calls=%async_computation.6 | async-start | bytes 32768 | tf_op jit(solution)/shard_map/all_to_all | solution.py:29
  395.7 3.4 multiply_subtract_fusion.3
  399.1 8.2 %all-to-all-done.6 = f32[32,1,6]{2,1,0:T(1,128)S(1)} async-done(((f32[32,1,6]{2,1,0:T(1,128)}), f32[32,1,6]{2,1,0:T(1,128)S(1)}, u32[]{:S(2)}, u32[]{:S(2)}) %all-to-all-start.6) | async-done | bytes 800 | tf_op jit(solution)/shard_map/all_to_all | solution.py:29
  417.1 2.7 multiply_subtract_fusion
  (524 shorter events, 134.1 us)
Async XLA Ops:
  1.8 9.2 %collective-permute-start.1 = (f32[1,3,2,1,32,256]{5,4,3,2,1,0:T(8,128)S(1)}, f32[1,3,2,1,32,256]{5,4,3,2,1,0:T(8,128)S(1)}, u32[]{:S(2)}, u32[]{:S(2)}) collective-permute-start(f32[1,3,2,1,32,256]{5,4,3,2,1,0:T(8,128)S(1)} %get-tuple-element.184), channel_id=1, source_target_pairs={{2,0},{4,2},{6,4},{8,6},{10,8},{12,10},{14,12},{16,14},{18,16},{20... | collective-permute-start | bytes 589832 | tf_op jit(solution)/shard_map/ppermute | solution.py:22
  3.1 7.8 %collective-permute-start = (f32[1,3,2,1,32,256]{5,4,3,2,1,0:T(8,128)S(1)}, f32[1,3,2,1,32,256]{5,4,3,2,1,0:T(8,128)S(1)}, u32[]{:S(2)}, u32[]{:S(2)}) collective-permute-start(f32[1,3,2,1,32,256]{5,4,3,2,1,0:T(8,128)S(1)} %get-tuple-element.185), channel_id=1, source_target_pairs={{0,2},{2,4},{4,6},{6,8},{8,10},{10,12},{12,14},{14,16},{16,18},{18... | collective-permute-start | bytes 589832 | tf_op jit(solution)/shard_map/ppermute | solution.py:19
  9.3 91.4 %copy-start.53 = (f32[1,1,1,1,256]{4,1,3,2,0:T(1,128)}, f32[1,1,1,1,256]{4,1,3,2,0:T(1,128)S(1)}, u32[]{:S(2)}) copy-start(f32[1,1,1,1,256]{4,1,3,2,0:T(1,128)S(1)} %get-tuple-element.352) | copy-start | bytes 3076
  10.4 174.5 %copy-start.10 = (f32[3,4,32,256]{3,2,1,0:T(8,128)}, f32[3,4,32,256]{3,2,1,0:T(8,128)S(1)}, u32[]{:S(2)}) copy-start(f32[3,4,32,256]{3,2,1,0:T(8,128)S(1)} %broadcast_multiply_fusion) | copy-start | bytes 1179652
  11.1 13.1 %collective-permute-start.2 = (f32[1,3,2,6,1,256]{5,4,3,2,1,0:T(1,128)S(1)}, f32[1,3,2,6,1,256]{5,4,3,2,1,0:T(1,128)S(1)}, u32[]{:S(2)}, u32[]{:S(2)}) collective-permute-start(f32[1,3,2,6,1,256]{5,4,3,2,1,0:T(1,128)S(1)} %get-tuple-element.134), channel_id=1, source_target_pairs={{1,0},{3,2},{5,4},{7,6},{9,8},{11,10},{13,12},{15,14},{17,16},{19,... | collective-permute-start | bytes 110600 | tf_op jit(solution)/shard_map/ppermute | solution.py:22
  22.9 3.1 collective-permute-start.3
  31.6 23.0 %all-to-all-start = ((f32[32,2,1]{1,2,0:T(1,128)}), f32[32,2,1]{1,2,0:T(1,128)S(1)}, u32[]{:S(2)}, u32[]{:S(2)}) async-start(f32[32,2,1]{1,2,0:T(1,128)} %broadcast_in_dim.76), calls=%async_computation | async-start | bytes 32768 | tf_op jit(solution)/shard_map/all_to_all | solution.py:29
  55.2 16.5 %all-to-all-start.1 = ((f32[32,2,1]{1,2,0:T(1,128)}), f32[32,2,1]{1,2,0:T(1,128)S(1)}, u32[]{:S(2)}, u32[]{:S(2)}) async-start(f32[32,2,1]{1,2,0:T(1,128)} %broadcast_in_dim.79), calls=%async_computation.1 | async-start | bytes 32768 | tf_op jit(solution)/shard_map/all_to_all | solution.py:29
  82.1 5.4 %collective-permute-start.4 = (f32[1,3,2,1,32,256]{5,4,3,2,1,0:T(8,128)S(1)}, f32[1,3,2,1,32,256]{5,4,3,2,1,0:T(8,128)S(1)}, u32[]{:S(2)}, u32[]{:S(2)}) collective-permute-start(f32[1,3,2,1,32,256]{5,4,3,2,1,0:T(8,128)S(1)} %get-tuple-element.180), channel_id=1, source_target_pairs={{0,2},{2,4},{4,6},{6,8},{8,10},{10,12},{12,14},{14,16},{16,18},{18... | collective-permute-start | bytes 589832 | tf_op jit(solution)/shard_map/ppermute | solution.py:19
  84.2 7.1 %collective-permute-start.5 = (f32[1,3,2,1,32,256]{5,4,3,2,1,0:T(8,128)S(1)}, f32[1,3,2,1,32,256]{5,4,3,2,1,0:T(8,128)S(1)}, u32[]{:S(2)}, u32[]{:S(2)}) collective-permute-start(f32[1,3,2,1,32,256]{5,4,3,2,1,0:T(8,128)S(1)} %get-tuple-element.181), channel_id=1, source_target_pairs={{2,0},{4,2},{6,4},{8,6},{10,8},{12,10},{14,12},{16,14},{18,16},{20... | collective-permute-start | bytes 589832 | tf_op jit(solution)/shard_map/ppermute | solution.py:22
  91.4 5.4 %collective-permute-start.7 = (f32[1,3,2,6,1,256]{5,4,3,2,1,0:T(1,128)S(1)}, f32[1,3,2,6,1,256]{5,4,3,2,1,0:T(1,128)S(1)}, u32[]{:S(2)}, u32[]{:S(2)}) collective-permute-start(f32[1,3,2,6,1,256]{5,4,3,2,1,0:T(1,128)S(1)} %get-tuple-element.133), channel_id=1, source_target_pairs={{0,1},{2,3},{4,5},{6,7},{8,9},{10,11},{12,13},{14,15},{16,17},{18,... | collective-permute-start | bytes 110600 | tf_op jit(solution)/shard_map/ppermute | solution.py:19
  92.7 4.9 %collective-permute-start.6 = (f32[1,3,2,6,1,256]{5,4,3,2,1,0:T(1,128)S(1)}, f32[1,3,2,6,1,256]{5,4,3,2,1,0:T(1,128)S(1)}, u32[]{:S(2)}, u32[]{:S(2)}) collective-permute-start(f32[1,3,2,6,1,256]{5,4,3,2,1,0:T(1,128)S(1)} %get-tuple-element.132), channel_id=1, source_target_pairs={{1,0},{3,2},{5,4},{7,6},{9,8},{11,10},{13,12},{15,14},{17,16},{19,... | collective-permute-start | bytes 110600 | tf_op jit(solution)/shard_map/ppermute | solution.py:22
  108.7 17.5 %all-to-all-start.2 = ((f32[32,1,6]{2,1,0:T(1,128)}), f32[32,1,6]{2,1,0:T(1,128)S(1)}, u32[]{:S(2)}, u32[]{:S(2)}) async-start(f32[32,1,6]{2,1,0:T(1,128)} %broadcast_in_dim.80), calls=%async_computation.2 | async-start | bytes 32768 | tf_op jit(solution)/shard_map/all_to_all | solution.py:29
  165.0 5.5 %collective-permute-start.8 = (f32[1,3,2,1,32,256]{5,4,3,2,1,0:T(8,128)S(1)}, f32[1,3,2,1,32,256]{5,4,3,2,1,0:T(8,128)S(1)}, u32[]{:S(2)}, u32[]{:S(2)}) collective-permute-start(f32[1,3,2,1,32,256]{5,4,3,2,1,0:T(8,128)S(1)} %get-tuple-element.168), channel_id=1, source_target_pairs={{0,2},{2,4},{4,6},{6,8},{8,10},{10,12},{12,14},{14,16},{16,18},{18... | collective-permute-start | bytes 589832 | tf_op jit(solution)/shard_map/ppermute | solution.py:19
  167.2 7.2 %collective-permute-start.9 = (f32[1,3,2,1,32,256]{5,4,3,2,1,0:T(8,128)S(1)}, f32[1,3,2,1,32,256]{5,4,3,2,1,0:T(8,128)S(1)}, u32[]{:S(2)}, u32[]{:S(2)}) collective-permute-start(f32[1,3,2,1,32,256]{5,4,3,2,1,0:T(8,128)S(1)} %get-tuple-element.169), channel_id=1, source_target_pairs={{2,0},{4,2},{6,4},{8,6},{10,8},{12,10},{14,12},{16,14},{18,16},{20... | collective-permute-start | bytes 589832 | tf_op jit(solution)/shard_map/ppermute | solution.py:22
  174.4 5.5 %collective-permute-start.11 = (f32[1,3,2,6,1,256]{5,4,3,2,1,0:T(1,128)S(1)}, f32[1,3,2,6,1,256]{5,4,3,2,1,0:T(1,128)S(1)}, u32[]{:S(2)}, u32[]{:S(2)}) collective-permute-start(f32[1,3,2,6,1,256]{5,4,3,2,1,0:T(1,128)S(1)} %get-tuple-element.131), channel_id=1, source_target_pairs={{0,1},{2,3},{4,5},{6,7},{8,9},{10,11},{12,13},{14,15},{16,17},{18,... | collective-permute-start | bytes 110600 | tf_op jit(solution)/shard_map/ppermute | solution.py:19
  175.7 4.9 %collective-permute-start.10 = (f32[1,3,2,6,1,256]{5,4,3,2,1,0:T(1,128)S(1)}, f32[1,3,2,6,1,256]{5,4,3,2,1,0:T(1,128)S(1)}, u32[]{:S(2)}, u32[]{:S(2)}) collective-permute-start(f32[1,3,2,6,1,256]{5,4,3,2,1,0:T(1,128)S(1)} %get-tuple-element.130), channel_id=1, source_target_pairs={{1,0},{3,2},{5,4},{7,6},{9,8},{11,10},{13,12},{15,14},{17,16},{19,... | collective-permute-start | bytes 110600 | tf_op jit(solution)/shard_map/ppermute | solution.py:22
  217.3 5.5 %collective-permute-start.12 = (f32[1,3,2,1,32,256]{5,4,3,2,1,0:T(8,128)S(1)}, f32[1,3,2,1,32,256]{5,4,3,2,1,0:T(8,128)S(1)}, u32[]{:S(2)}, u32[]{:S(2)}) collective-permute-start(f32[1,3,2,1,32,256]{5,4,3,2,1,0:T(8,128)S(1)} %get-tuple-element.162), channel_id=1, source_target_pairs={{0,2},{2,4},{4,6},{6,8},{8,10},{10,12},{12,14},{14,16},{16,18},{18... | collective-permute-start | bytes 589832 | tf_op jit(solution)/shard_map/ppermute | solution.py:19
  219.5 7.2 %collective-permute-start.13 = (f32[1,3,2,1,32,256]{5,4,3,2,1,0:T(8,128)S(1)}, f32[1,3,2,1,32,256]{5,4,3,2,1,0:T(8,128)S(1)}, u32[]{:S(2)}, u32[]{:S(2)}) collective-permute-start(f32[1,3,2,1,32,256]{5,4,3,2,1,0:T(8,128)S(1)} %get-tuple-element.163), channel_id=1, source_target_pairs={{2,0},{4,2},{6,4},{8,6},{10,8},{12,10},{14,12},{16,14},{18,16},{20... | collective-permute-start | bytes 589832 | tf_op jit(solution)/shard_map/ppermute | solution.py:22
  226.7 5.4 %collective-permute-start.15 = (f32[1,3,2,6,1,256]{5,4,3,2,1,0:T(1,128)S(1)}, f32[1,3,2,6,1,256]{5,4,3,2,1,0:T(1,128)S(1)}, u32[]{:S(2)}, u32[]{:S(2)}) collective-permute-start(f32[1,3,2,6,1,256]{5,4,3,2,1,0:T(1,128)S(1)} %get-tuple-element.129), channel_id=1, source_target_pairs={{0,1},{2,3},{4,5},{6,7},{8,9},{10,11},{12,13},{14,15},{16,17},{18,... | collective-permute-start | bytes 110600 | tf_op jit(solution)/shard_map/ppermute | solution.py:19
  228.1 4.9 %collective-permute-start.14 = (f32[1,3,2,6,1,256]{5,4,3,2,1,0:T(1,128)S(1)}, f32[1,3,2,6,1,256]{5,4,3,2,1,0:T(1,128)S(1)}, u32[]{:S(2)}, u32[]{:S(2)}) collective-permute-start(f32[1,3,2,6,1,256]{5,4,3,2,1,0:T(1,128)S(1)} %get-tuple-element.128), channel_id=1, source_target_pairs={{1,0},{3,2},{5,4},{7,6},{9,8},{11,10},{13,12},{15,14},{17,16},{19,... | collective-permute-start | bytes 110600 | tf_op jit(solution)/shard_map/ppermute | solution.py:22
  244.2 17.7 %all-to-all-start.4 = ((f32[32,1,6]{2,1,0:T(1,128)}), f32[32,1,6]{2,1,0:T(1,128)S(1)}, u32[]{:S(2)}, u32[]{:S(2)}) async-start(f32[32,1,6]{2,1,0:T(1,128)} %broadcast_in_dim.82), calls=%async_computation.4 | async-start | bytes 32768 | tf_op jit(solution)/shard_map/all_to_all | solution.py:29
  303.1 5.5 %collective-permute-start.16 = (f32[1,3,2,1,32,256]{5,4,3,2,1,0:T(8,128)S(1)}, f32[1,3,2,1,32,256]{5,4,3,2,1,0:T(8,128)S(1)}, u32[]{:S(2)}, u32[]{:S(2)}) collective-permute-start(f32[1,3,2,1,32,256]{5,4,3,2,1,0:T(8,128)S(1)} %get-tuple-element.150), channel_id=1, source_target_pairs={{0,2},{2,4},{4,6},{6,8},{8,10},{10,12},{12,14},{14,16},{16,18},{18... | collective-permute-start | bytes 589832 | tf_op jit(solution)/shard_map/ppermute | solution.py:19
  305.2 7.2 %collective-permute-start.17 = (f32[1,3,2,1,32,256]{5,4,3,2,1,0:T(8,128)S(1)}, f32[1,3,2,1,32,256]{5,4,3,2,1,0:T(8,128)S(1)}, u32[]{:S(2)}, u32[]{:S(2)}) collective-permute-start(f32[1,3,2,1,32,256]{5,4,3,2,1,0:T(8,128)S(1)} %get-tuple-element.151), channel_id=1, source_target_pairs={{2,0},{4,2},{6,4},{8,6},{10,8},{12,10},{14,12},{16,14},{18,16},{20... | collective-permute-start | bytes 589832 | tf_op jit(solution)/shard_map/ppermute | solution.py:22
  312.5 5.5 %collective-permute-start.19 = (f32[1,3,2,6,1,256]{5,4,3,2,1,0:T(1,128)S(1)}, f32[1,3,2,6,1,256]{5,4,3,2,1,0:T(1,128)S(1)}, u32[]{:S(2)}, u32[]{:S(2)}) collective-permute-start(f32[1,3,2,6,1,256]{5,4,3,2,1,0:T(1,128)S(1)} %get-tuple-element.127), channel_id=1, source_target_pairs={{0,1},{2,3},{4,5},{6,7},{8,9},{10,11},{12,13},{14,15},{16,17},{18,... | collective-permute-start | bytes 110600 | tf_op jit(solution)/shard_map/ppermute | solution.py:19
  313.8 4.8 %collective-permute-start.18 = (f32[1,3,2,6,1,256]{5,4,3,2,1,0:T(1,128)S(1)}, f32[1,3,2,6,1,256]{5,4,3,2,1,0:T(1,128)S(1)}, u32[]{:S(2)}, u32[]{:S(2)}) collective-permute-start(f32[1,3,2,6,1,256]{5,4,3,2,1,0:T(1,128)S(1)} %get-tuple-element.126), channel_id=1, source_target_pairs={{1,0},{3,2},{5,4},{7,6},{9,8},{11,10},{13,12},{15,14},{17,16},{19,... | collective-permute-start | bytes 110600 | tf_op jit(solution)/shard_map/ppermute | solution.py:22
  328.2 17.7 %all-to-all-start.5 = ((f32[32,2,1]{1,2,0:T(1,128)}), f32[32,2,1]{1,2,0:T(1,128)S(1)}, u32[]{:S(2)}, u32[]{:S(2)}) async-start(f32[32,2,1]{1,2,0:T(1,128)} %broadcast_in_dim.83), calls=%async_computation.5 | async-start | bytes 32768 | tf_op jit(solution)/shard_map/all_to_all | solution.py:29
  357.9 6.0 %collective-permute-start.20 = (f32[1,3,2,1,32,256]{5,4,3,2,1,0:T(8,128)S(1)}, f32[1,3,2,1,32,256]{5,4,3,2,1,0:T(8,128)S(1)}, u32[]{:S(2)}, u32[]{:S(2)}) collective-permute-start(f32[1,3,2,1,32,256]{5,4,3,2,1,0:T(8,128)S(1)} %get-tuple-element.144), channel_id=1, source_target_pairs={{0,2},{2,4},{4,6},{6,8},{8,10},{10,12},{12,14},{14,16},{16,18},{18... | collective-permute-start | bytes 589832 | tf_op jit(solution)/shard_map/ppermute | solution.py:19
  360.2 7.3 %collective-permute-start.21 = (f32[1,3,2,1,32,256]{5,4,3,2,1,0:T(8,128)S(1)}, f32[1,3,2,1,32,256]{5,4,3,2,1,0:T(8,128)S(1)}, u32[]{:S(2)}, u32[]{:S(2)}) collective-permute-start(f32[1,3,2,1,32,256]{5,4,3,2,1,0:T(8,128)S(1)} %get-tuple-element.145), channel_id=1, source_target_pairs={{2,0},{4,2},{6,4},{8,6},{10,8},{12,10},{14,12},{16,14},{18,16},{20... | collective-permute-start | bytes 589832 | tf_op jit(solution)/shard_map/ppermute | solution.py:22
  367.6 7.7 %collective-permute-start.23 = (f32[1,3,2,6,1,256]{5,4,3,2,1,0:T(1,128)S(1)}, f32[1,3,2,6,1,256]{5,4,3,2,1,0:T(1,128)S(1)}, u32[]{:S(2)}, u32[]{:S(2)}) collective-permute-start(f32[1,3,2,6,1,256]{5,4,3,2,1,0:T(1,128)S(1)} %get-tuple-element.125), channel_id=1, source_target_pairs={{0,1},{2,3},{4,5},{6,7},{8,9},{10,11},{12,13},{14,15},{16,17},{18,... | collective-permute-start | bytes 110600 | tf_op jit(solution)/shard_map/ppermute | solution.py:19
  371.2 4.8 %collective-permute-start.22 = (f32[1,3,2,6,1,256]{5,4,3,2,1,0:T(1,128)S(1)}, f32[1,3,2,6,1,256]{5,4,3,2,1,0:T(1,128)S(1)}, u32[]{:S(2)}, u32[]{:S(2)}) collective-permute-start(f32[1,3,2,6,1,256]{5,4,3,2,1,0:T(1,128)S(1)} %get-tuple-element.124), channel_id=1, source_target_pairs={{1,0},{3,2},{5,4},{7,6},{9,8},{11,10},{13,12},{15,14},{17,16},{19,... | collective-permute-start | bytes 110600 | tf_op jit(solution)/shard_map/ppermute | solution.py:22
  389.5 17.7 %all-to-all-start.6 = ((f32[32,1,6]{2,1,0:T(1,128)}), f32[32,1,6]{2,1,0:T(1,128)S(1)}, u32[]{:S(2)}, u32[]{:S(2)}) async-start(f32[32,1,6]{2,1,0:T(1,128)} %broadcast_in_dim.84), calls=%async_computation.6 | async-start | bytes 32768 | tf_op jit(solution)/shard_map/all_to_all | solution.py:29
  (119 other events, 868.1 us)
where the time goes:
time: 428 us; the launch traced here: 425 us
  starting transfers between devices  105 us (25%)
  between operations  100 us (23%)
  waiting for transfers between devices  89 us (21%)
  other arithmetic  76.9 us (18%)
  local copies, waits for them, and re-layouts  36.4 us (9%)
  blocking collectives  17.5 us (4%)
    all_to_all x6, waiting for transfers between devices, sent_to_all(): return lax.all_to_all(copies, axis, split_axis=0, concat_axis=0, tiled=True)  56.8 us
    all_to_all x6, starting transfers between devices, sent_to_all(): return lax.all_to_all(copies, axis, split_axis=0, concat_axis=0, tiled=True)  40.5 us
    ppermute x12, starting transfers between devices, with_halo(): lax.ppermute(lax.slice_in_dim(block, 0, width, axis=dim), axis, backward)  40.2 us
    sub x15, other arithmetic, scaled(): real_part = values[:, :, 0] * real_scale - values[:, :, 1] * imag_scale  27.6 us
    ppermute x12, starting transfers between devices, with_halo(): lax.ppermute(lax.slice_in_dim(block, block.shape[dim] - width, None, axis...  24.1 us
    ppermute x12, waiting for transfers between devices, with_halo(): lax.ppermute(lax.slice_in_dim(block, 0, width, axis=dim), axis, backward)  22 us
    all_to_all x1, blocking collectives, sent_to_all(): return lax.all_to_all(copies, axis, split_axis=0, concat_axis=0, tiled=True)  17.5 us
    unnamed x244, local copies, waits for them, and re-layouts  15.5 us
  transfers between devices with their start and end apart: 30, of which 22 were waited for; matrix products, arithmetic and copies ran while one was open for 3% of the time, Pallas kernels for 0%

commit v1 on v0

v1 whole, which is shorter than its diff:
```python
import functools

import jax
import jax.numpy as jnp
from jax import lax
from jax.experimental import pallas as pl
from jax.experimental.pallas import tpu as pltpu
from jax.sharding import PartitionSpec as P

PML = 8
ITERS = 3
DEGREE = 2 * ITERS
pml_strength = 2.0
LANES = 128
TILE = 8

NODES = (0.0, -1.0, 1.0, 0.577, -0.671, 0.319)
F32 = jnp.float32
VMEM = pl.BlockSpec(memory_space=pltpu.VMEM)
ANY = pl.BlockSpec(memory_space=pl.ANY)


def params(mib):
    return pltpu.CompilerParams(vmem_limit_bytes=mib * 2**20)


def stretch(points, length, frequency):
    inside = jnp.maximum(jnp.maximum(PML - points, points - (length - PML)), 0.0) / PML
    damping = pml_strength * inside * inside * inside / frequency
    factor = 1.0 / (1.0 + damping * damping)
    return factor, -damping * factor


def times(value, factor):
    return (
        value[0] * factor[0] - value[1] * factor[1],
        value[0] * factor[1] + value[1] * factor[0],
    )


def minus(a, b):
    return a[0] - b[0], a[1] - b[1]


def plus(a, b):
    return a[0] + b[0], a[1] + b[1]


def iota(shape, axis):
    return lax.broadcasted_iota(jnp.int32, shape, axis)


class Line:
    def __init__(self):
        self.lane = iota((TILE, LANES), 1)
        self.row = iota((TILE, LANES), 0)
        self.zero = jnp.zeros((TILE, LANES), F32)

    def z_next(self, low, high):
        low, high = pltpu.roll(low, LANES - 1, 1), pltpu.roll(high, LANES - 1, 1)
        last = self.lane == LANES - 1
        return jnp.where(last, high, low), jnp.where(last, 0.0, high)

    def z_before(self, low, high):
        low, high = pltpu.roll(low, 1, 1), pltpu.roll(high, 1, 1)
        first = self.lane == 0
        return jnp.where(first, 0.0, low), jnp.where(first, low, high)

    def up(self, tile):
        return pltpu.roll(tile, TILE - 1, 0)

    def down(self, tile):
        return pltpu.roll(tile, 1, 0)

    def y_next(self, rolled, rolled_after):
        return jnp.where(self.row == TILE - 1, rolled_after, rolled)

    def y_before(self, rolled, rolled_ahead):
        return jnp.where(self.row == 0, rolled_ahead, rolled)


def z_steps(line, pair):
    out = []
    for part in range(2):
        low, high = pair[0][part], pair[1][part]
        a, b = line.z_next(low, high)
        out.append((a - low, b - high))
    return [(out[0][h], out[1][h]) for h in range(2)]


def z_steps_back(line, pair):
    out = []
    for part in range(2):
        low, high = pair[0][part], pair[1][part]
        a, b = line.z_before(low, high)
        out.append((low - a, high - b))
    return [(out[0][h], out[1][h]) for h in range(2)]


def row_of(ref, at):
    return jnp.broadcast_to(ref[at : at + 1, :], (TILE, LANES))


def complex_row(ref, at):
    return row_of(ref, at), row_of(ref, at + 1)


def is_stretched(t, tiles):
    return t * TILE < PML or (t + 1) * TILE > tiles * TILE - PML


def edge_terms(line, field, t, tiles, fz, fx, y_front, store):
    now = field(t)
    after = field(t + 1) if t + 1 < tiles else None
    dz = z_steps(line, now[0])
    for h in range(2):
        gy = plus(times(dz[h], fz[h]), times(now[2][h], fx))
        dy = []
        for part in range(2):
            rolled = line.up(now[0][h][part])
            nxt = line.up(after[0][h][part]) if after is not None else line.zero
            dy.append(line.y_next(rolled, nxt) - now[0][h][part])
        if is_stretched(t, tiles):
            dy = times(dy, y_front(t))
        gz = minus((-dy[0], -dy[1]), times(now[1][h], fx))
        for part in range(2):
            store(0, part, h, t, gy[part])
            store(1, part, h, t, gz[part])


def tile_reader(ref, components=3):
    def read(t):
        s = slice(t * TILE, (t + 1) * TILE)
        return [
            [(ref[c, 0, h, s, :], ref[c, 1, h, s, :]) for h in range(2)] for c in range(components)
        ]

    return read


def tile_writer(ref):
    def write(c, part, h, t, value):
        ref[c, part, h, t * TILE : (t + 1) * TILE, :] = value

    return write


def start_kernel(
    cells_x, src, eps, src_in, eps_in, freq,
    o_ref, n_ref, mo_ref, mn_ref, go_ref, gn_ref, off_ref, on_ref, cy_ref, cz_ref, cx_ref, ct_ref,
):
    core = lax.axis_index("gy")
    chip = lax.axis_index("gx")
    rows, cols = src.shape[4], src.shape[5]
    ny, nx = 2 * rows, cells_x * lax.axis_size("gx")
    half_x = cells_x // 2
    tiles = ny // TILE
    f = jnp.broadcast_to(freq[...], (TILE, LANES))
    square = f * f

    def arrange(first_own):
        own_rows = slice(rows * first_own, rows * (first_own + 1))
        other_rows = slice(rows * (1 - first_own), rows * (2 - first_own))
        for dest, mdest, plane in ((o_ref, mo_ref, first_own), (n_ref, mn_ref, 1 - first_own)):
            for h in range(2):
                z = slice(h * LANES, (h + 1) * LANES)
                for c in range(3):
                    for part in range(2):
                        dest[c, part, h, own_rows, :] = src[0, c, part, half_x * first_own + plane, :, z]
                        dest[c, part, h, other_rows, :] = src_in[c, part, plane, :, z]
                    scale = square[0:1, :]
                    mdest[c, h, own_rows, :] = eps[c, half_x * first_own + plane, :, z] * scale
                    mdest[c, h, other_rows, :] = eps_in[c, plane, :, z] * scale

    @pl.when(core == 0)
    def _():
        arrange(0)

    @pl.when(core != 0)
    def _():
        arrange(1)

    fy = jnp.broadcast_to(freq[...], (ny, LANES))
    y = iota((ny, LANES), 0).astype(F32)
    cy_ref[0], cy_ref[1] = stretch(y + 0.5, ny, fy)
    cy_ref[2], cy_ref[3] = stretch(y, ny, fy)
    lane = iota((TILE, LANES), 1)
    for h in range(2):
        z = (lane + h * LANES).astype(F32)
        for i, value in enumerate((*stretch(z + 0.5, cols, f), *stretch(z, cols, f))):
            cz_ref[4 * h + i : 4 * h + i + 1, :] = value[0:1, :]
    base = chip * cells_x + core * half_x
    for at, plane in ((0, core), (TILE, 1 - core)):
        x = (jnp.zeros((TILE, LANES), jnp.int32) + (base + plane)).astype(F32)
        values = (*stretch(x - 0.5, nx, f), *stretch(x + 0.5, nx, f), *stretch(x, nx, f))
        for i, value in enumerate(values):
            cx_ref[at + i : at + i + 1, :] = value[0:1, :]
    low = square * -12.0
    centre, radius = (12.0 + low) * 0.5, (12.0 - low) * 0.5
    for k, node in enumerate(NODES):
        ct_ref[k : k + 1, :] = (centre + radius * node)[0:1, :]
    ct_ref[DEGREE : DEGREE + 1, :] = (2.0 / radius)[0:1, :]

    line = Line()
    fz = [complex_row(cz_ref, 4 * h) for h in range(2)]

    def y_front(t):
        s = slice(t * TILE, (t + 1) * TILE)
        return cy_ref[0, s, :], cy_ref[1, s, :]

    for ref, g_ref, at in ((o_ref, go_ref, 0), (n_ref, gn_ref, TILE)):
        for t in range(tiles):
            edge_terms(
                line, tile_reader(ref), t, tiles, fz, complex_row(cx_ref, at + 2), y_front,
                tile_writer(g_ref),
            )

    @pl.when(core == 0)
    def _():
        off_ref[...] = o_ref[1:3]
        on_ref[...] = gn_ref[...]

    @pl.when(core != 0)
    def _():
        off_ref[...] = go_ref[...]
        on_ref[...] = n_ref[1:3]


def plane_kernel(
    outer, k, p_ref, q_ref, gq_ref, halo_ref, m_ref, cy_ref, cz_ref, cx_ref, ct_ref,
    new_ref, g_ref, out_ref,
):
    core = lax.axis_index("gy")
    chip = lax.axis_index("gx")
    tiles = p_ref.shape[3] // TILE
    at = 0 if outer else TILE
    line = Line()
    before = complex_row(cx_ref, at)
    fx = complex_row(cx_ref, at + 2)
    bx = complex_row(cx_ref, at + 4)
    fz = [complex_row(cz_ref, 4 * h) for h in range(2)]
    bz = [complex_row(cz_ref, 4 * h + 2) for h in range(2)]
    node = row_of(ct_ref, k)
    scale = row_of(ct_ref, DEGREE)

    def y_factor(first, t):
        s = slice(t * TILE, (t + 1) * TILE)
        return cy_ref[first, s, :], cy_ref[first + 1, s, :]

    def run(left):
        zero = line.zero
        edge = left and outer
        wall = outer and not left
        at_edge = (chip == 0) if edge else (chip == lax.axis_size("gx") - 1)
        closed = jnp.zeros((TILE, LANES), jnp.int32) + at_edge.astype(jnp.int32) > 0
        read_p = tile_reader(p_ref)
        read_g = tile_reader(halo_ref if left else gq_ref, 2)
        if left:
            read_r = lambda t: tile_reader(q_ref)(t)[1:]
        else:
            read_r = tile_reader(halo_ref, 2)
        rolled_h = None
        pending = None
        nxt = read_p(0)
        rolled = [[[line.up(nxt[c][h][i]) for i in range(2)] for h in range(2)] for c in (0, 2)]
        write_new, write_g, write_out = tile_writer(new_ref), tile_writer(g_ref), tile_writer(out_ref)
        write_edge = write_g if left else write_out

        def finish(pend, after):
            t0, ex, rolled_ex, base = pend
            for h in range(2):
                dy = [
                    line.y_next(rolled_ex[h][i], after[h][i] if after is not None else zero) - ex[h][i]
                    for i in range(2)
                ]
                if is_stretched(t0, tiles):
                    dy = times(dy, y_factor(0, t0))
                for i in range(2):
                    write_edge(1, i, h, t0, base[h][i] - dy[i])

        for t in range(tiles):
            ex, ey, ez = nxt
            if t + 1 < tiles:
                nxt = read_p(t + 1)
                rolled_next = [
                    [[line.up(nxt[c][h][i]) for i in range(2)] for h in range(2)] for c in (0, 2)
                ]
            else:
                rolled_next = [[[zero] * 2] * 2] * 2
            gl, right = read_g(t), read_r(t)
            pml = is_stretched(t, tiles)
            dz_y, dz_x = z_steps(line, ey), z_steps(line, ex)
            hx, hy, hz, cross_y, cross_z = [], [], [], [], []
            for h in range(2):
                dy_x, dy_z = (
                    [
                        line.y_next(rolled[j][h][i], rolled_next[j][h][i]) - field[h][i]
                        for i in range(2)
                    ]
                    for j, field in ((0, ex), (1, ez))
                )
                if pml:
                    dy_x, dy_z = times(dy_x, y_factor(0, t)), times(dy_z, y_factor(0, t))
                r_y, r_z = right[0][h], right[1][h]
                if wall:
                    r_y = [jnp.where(closed, 0.0, r) for r in r_y]
                    r_z = [jnp.where(closed, 0.0, r) for r in r_z]
                hx.append(minus(dy_z, times(dz_y[h], fz[h])))
                hy.append(minus(times(dz_x[h], fz[h]), times(minus(r_z, ez[h]), fx)))
                hz.append(minus(times(minus(r_y, ey[h]), fx), dy_x))
                l_y = minus(gl[0][h], times(ez[h], before))
                l_z = plus(gl[1][h], times(ey[h], before))
                if edge:
                    l_y = [jnp.where(closed, 0.0, v) for v in l_y]
                    l_z = [jnp.where(closed, 0.0, v) for v in l_z]
                cross_y.append(times(minus(hy[h], l_y), bx))
                cross_z.append(times(minus(hz[h], l_z), bx))
            rolled = rolled_next
            new_rolled = [[[line.down(v[h][i]) for i in range(2)] for h in range(2)] for v in (hx, hz)]
            bz_y, bz_x = z_steps_back(line, hy), z_steps_back(line, hx)
            s = slice(t * TILE, (t + 1) * TILE)
            made = [[], [], []]
            for h in range(2):
                by_x, by_z = (
                    [
                        field[h][i]
                        - line.y_before(
                            new_rolled[j][h][i], rolled_h[j][h][i] if rolled_h is not None else zero
                        )
                        for i in range(2)
                    ]
                    for j, field in ((0, hx), (1, hz))
                )
                if pml:
                    by_x, by_z = times(by_x, y_factor(2, t)), times(by_z, y_factor(2, t))
                curls = (
                    minus(by_z, times(bz_y[h], bz[h])),
                    minus(times(bz_x[h], bz[h]), cross_z[h]),
                    minus(cross_y[h], by_x),
                )
                for c, (curl, field) in enumerate(zip(curls, (ex, ey, ez))):
                    shifted = m_ref[c, h, s, :] + node
                    made[c].append([(curl[i] - shifted * field[h][i]) * scale for i in range(2)])
                    for i in range(2):
                        write_new(c, i, h, t, made[c][h][i])
                        if left and c:
                            write_out(c - 1, i, h, t, made[c][h][i])
            rolled_h = new_rolled
            dz = z_steps(line, made[0])
            up = [[line.up(made[0][h][i]) for i in range(2)] for h in range(2)]
            base = []
            for h in range(2):
                gy = plus(times(dz[h], fz[h]), times(made[2][h], fx))
                for i in range(2):
                    write_edge(0, i, h, t, gy[i])
                b = times(made[1][h], fx)
                base.append((-b[0], -b[1]))
            if pending is not None:
                finish(pending, up)
            pending = (t, made[0], up, base)
        finish(pending, None)

    left_here = (core == 0) if outer else (core != 0)

    @pl.when(left_here)
    def _():
        run(True)

    @pl.when(jnp.logical_not(left_here))
    def _():
        run(False)


def two_sum(a, b):
    s = a + b
    v = s - a
    return s, (a - (s - v)) + (b - v)


def total_of(tile):
    top = jnp.max(jnp.max(jnp.abs(tile), axis=1, keepdims=True), axis=0, keepdims=True)
    shift = top * 1024.0
    lead = (tile + shift) - shift
    rest = tile - lead
    add = lambda v: jnp.sum(jnp.sum(v, axis=1, keepdims=True), axis=0, keepdims=True)
    return add(lead), add(rest)


def gram_kernel(k, copies, *refs):
    count = k + 1
    os, ns = refs[:count], refs[count : 2 * count]
    rest = list(refs[2 * count :])
    row_in = rest.pop(0) if k else None
    row_ref = rest.pop(0)
    core = lax.axis_index("gy")
    tiles = os[0].shape[3] // TILE
    zero = jnp.zeros((TILE, LANES), F32)
    real = [[zero, zero] for _ in range(count)]
    imag = [[zero, zero] for _ in range(count)]
    for which, group in enumerate((os, ns)):
        for c in range(3):
            for h in range(2):
                for t in range(tiles):
                    s = slice(t * TILE, (t + 1) * TILE)
                    ar, ai = group[k][c, 0, h, s, :], group[k][c, 1, h, s, :]
                    for i in range(k):
                        br, bi = group[i][c, 0, h, s, :], group[i][c, 1, h, s, :]
                        real[i][which] += br * ar + bi * ai
                        imag[i][which] += br * ai - bi * ar
                    real[k][which] += ar * ar + ai * ai
    lane = iota((1, LANES), 1)
    row = row_in[...] if k else jnp.zeros((1, LANES), F32)
    for i in range(count):
        lead, less = total_of(real[i][0] + real[i][1])
        row = jnp.where(lane == 8 * i + k, lead, row)
        row = jnp.where(lane == 64 + 8 * i + k, less, row)
        if i < k:
            lead, less = total_of(imag[i][0] + imag[i][1])
            row = jnp.where(lane == 8 * k + i, lead, row)
            row = jnp.where(lane == 64 + 8 * k + i, less, row)
    if copies == 1:
        row_ref[...] = row
    else:
        for d in range(copies):
            row_ref[d] = row
    if k:
        other_ref = rest.pop(0)
        half = other_ref.shape[4]
        first = pl.multiple_of(half * (1 - core), TILE)
        for which, group in enumerate((os, ns)):
            for c in range(3):
                for part in range(2):
                    for h in range(2):
                        other_ref[which, c, part, h] = group[k][c, part, h, pl.ds(first, half), :]


def quick(a, b):
    s = a + b
    return s, b - (s - a)


def add2(a, b):
    s, e = two_sum(a[0], b[0])
    return quick(s, e + (a[1] + b[1]))


def neg2(a):
    return -a[0], -a[1]


def split(a):
    c = a * 4097.0
    high = c - (c - a)
    return high, a - high


def mul2(a, b):
    p = a[0] * b[0]
    (a1, a2), (b1, b2) = split(a[0]), split(b[0])
    e = ((a1 * b1 - p) + a1 * b2 + a2 * b1) + a2 * b2
    return quick(p, e + (a[0] * b[1] + a[1] * b[0]))


def div2(a, b):
    q = a[0] / b[0]
    rest = add2(a, neg2(mul2((q, jnp.zeros_like(q)), b)))
    q2 = rest[0] / b[0]
    rest = add2(rest, neg2(mul2((q2, jnp.zeros_like(q)), b)))
    return add2(quick(q, q2), (rest[0] / b[0], jnp.zeros_like(q)))


def cadd(a, b):
    return add2(a[0], b[0]), add2(a[1], b[1])


def cneg(a):
    return neg2(a[0]), neg2(a[1])


def conj(a):
    return a[0], neg2(a[1])


def cmul(a, b):
    return (
        add2(mul2(a[0], b[0]), neg2(mul2(a[1], b[1]))),
        add2(mul2(a[0], b[1]), mul2(a[1], b[0])),
    )


def cdiv(a, b):
    size = add2(mul2(b[0], b[0]), mul2(b[1], b[1]))
    top = cmul(a, conj(b))
    return div2(top[0], size), div2(top[1], size)


def each(fn, a):
    return tuple((fn(p[0]), fn(p[1])) for p in a)


def over_rows(a):
    for d in (4, 2, 1):
        a = cadd(a, each(lambda v: pltpu.roll(v, d, 0), a))
    return a


def coefficients(gathered, ct_ref):
    parts = [gathered[i * TILE : (i + 1) * TILE] for i in range(gathered.shape[0] // TILE)]
    parts = [(p, jnp.zeros_like(p)) for p in parts]
    while len(parts) > 1:
        parts = [add2(parts[2 * i], parts[2 * i + 1]) for i in range(len(parts) // 2)]
    total = parts[0]
    for d in (4, 2, 1):
        total = add2(total, tuple(pltpu.roll(v, d, 0) for v in total))
    other = tuple(pltpu.roll(v, 64, 1) for v in total)
    total = add2(total, other)
    row, lane = iota((TILE, LANES), 0), iota((TILE, LANES), 1)

    def picked(mask):
        return tuple(
            jnp.broadcast_to(
                jnp.sum(jnp.where(mask, v, 0.0), axis=1, keepdims=True), (TILE, LANES)
            )
            for v in total
        )

    columns = []
    for j in range(DEGREE + 1):
        real = picked(lane == 8 * jnp.minimum(row, j) + jnp.maximum(row, j))
        imag = picked((lane == 8 * jnp.maximum(row, j) + jnp.minimum(row, j)) & (row != j))
        imag = tuple(jnp.where(row > j, -v, v) for v in imag)
        columns.append((real, imag))
    zero = jnp.zeros((TILE, LANES), F32)
    first_row = conj(columns[0])
    scale = row_of(ct_ref, DEGREE)
    node = zero
    for k in range(DEGREE):
        node = jnp.where(row == k, row_of(ct_ref, k), node)
    node = mul2((node, zero), (scale, zero))

    def applied(c):
        return cadd(
            each(lambda v: pltpu.roll(v, 1, 0), c), (mul2(c[0], node), mul2(c[1], node))
        )

    def dot(a, b):
        return over_rows(cmul(conj(a), b))

    def with_first(c):
        return over_rows(cmul(first_row, c))

    def through_gram(c, count):
        out = None
        for j in range(count):
            term = cmul(columns[j], each(lambda v: jnp.broadcast_to(v[j : j + 1, :], (TILE, LANES)), c))
            out = term if out is None else cadd(out, term)
        return out

    one = jnp.where(row == 0, 1.0, 0.0).astype(F32)
    unit = ((one, zero), (zero, zero))
    nothing = ((zero, zero), (zero, zero))
    solution, residual, direction = nothing, unit, unit
    rho = with_first(unit)
    for iteration in range(ITERS):
        image = applied(direction)
        alpha = cdiv(rho, with_first(image))
        middle = cadd(residual, cneg(cmul(alpha, image)))
        second = applied(middle)
        weighted = through_gram(second, 2 * iteration + 3)
        size = dot(second, weighted)
        size = (size[0], (zero, zero))
        along = conj(dot(middle, weighted))
        weight = (div2(along[0], size[0]), div2(along[1], size[0]))
        solution = cadd(solution, cadd(cmul(alpha, direction), cmul(weight, middle)))
        residual = cadd(middle, cneg(cmul(weight, second)))
        if iteration + 1 < ITERS:
            following = cneg(cmul(weight, with_first(second)))
            beta = cmul(cdiv(following, rho), cdiv(alpha, weight))
            direction = cadd(
                residual, cmul(beta, cadd(direction, cneg(cmul(weight, image))))
            )
            rho = following
    solution = tuple(mul2(v, (scale, zero)) for v in solution)
    return solution, residual


def last_step_kernel(*refs):
    gathered, ct_ref, src = refs[:3]
    os, ns, xs = refs[3:9], refs[9:15], refs[15:21]
    x_hbm, r_hbm, x_ref, r_ref, sems = refs[21:]
    core = lax.axis_index("gy")
    half = src.shape[4]
    solution, residual = coefficients(gathered[:, 0, :], ct_ref)

    def spread(value):
        return [
            tuple(jnp.broadcast_to(part[0][j : j + 1, :], (TILE, LANES)) for part in value)
            for j in range(DEGREE + 1)
        ]

    cs, cr = spread(solution), spread(residual)
    own = half * core
    copies = []
    for c in range(3):
        for plane, refs_of, which, shift in (
            (3 * core, os, None, own),
            (1 + core, ns, None, own),
            (3 * (1 - core), xs, 0, 0),
            (2 - core, xs, 1, 0),
        ):
            for t in range(half // TILE):
                s = slice(t * TILE, (t + 1) * TILE)
                for h in range(2):
                    z = slice(h * LANES, (h + 1) * LANES)
                    vr, vi = src[0, c, 0, plane, s, z], src[0, c, 1, plane, s, z]
                    sol = times((vr, vi), cs[0])
                    res = times((vr, vi), cr[0])
                    for k in range(1, DEGREE + 1):
                        ref = refs_of[k - 1]
                        if which is None:
                            at = pl.ds(pl.multiple_of(shift + t * TILE, TILE), TILE)
                            v = ref[c, 0, h, at, :], ref[c, 1, h, at, :]
                        else:
                            v = ref[which, c, 0, h, s, :], ref[which, c, 1, h, s, :]
                        res = plus(res, times(v, cr[k]))
                        if k < DEGREE:
                            sol = plus(sol, times(v, cs[k]))
                    for part in range(2):
                        x_ref[c, part, plane, s, z] = sol[part]
                        r_ref[c, part, plane, s, z] = res[part]
        for n, (a, b) in enumerate(((x_ref, x_hbm), (r_ref, r_hbm))):
            copy = pltpu.make_async_copy(a.at[c], b.at[0, c], sems.at[n, c])
            copy.start()
            copies.append(copy)
    for copy in copies:
        copy.wait()


def body(source, permittivity, frequency):
    cells_x, rows, depth = source.shape[3:]
    chips = lax.axis_size("gx")
    core = lax.axis_index("gy")
    both = [(0, 1), (1, 0)]
    ring = [(2 * i + 1, (2 * i + 2) % (2 * chips)) for i in range(chips)]
    ring = ring + [(b, a) for a, b in ring]

    def shape(*dims):
        return jax.ShapeDtypeStruct(dims, F32)

    def cost(flops):
        return pl.CostEstimate(flops=flops, bytes_accessed=0, transcendentals=0)

    half_x = cells_x // 2
    away = half_x * (1 - core)
    src_in = lax.ppermute(
        lax.dynamic_slice_in_dim(source[0], away, half_x, axis=2), "gy", both
    )
    eps_in = lax.ppermute(
        lax.dynamic_slice_in_dim(permittivity, away, half_x, axis=1), "gy", both
    )
    ny = 2 * rows
    field, pair = shape(3, 2, 2, ny, LANES), shape(2, 2, 2, ny, LANES)
    medium = shape(3, 2, ny, LANES)
    o, n, mo, mn, go, gn, off, on, cy, cz, cx, ct = pl.pallas_call(
        functools.partial(start_kernel, cells_x),
        out_shape=[
            field, field, medium, medium, pair, pair, pair, pair,
            shape(4, ny, LANES), shape(TILE, LANES), shape(2 * TILE, LANES), shape(TILE, LANES),
        ],
        in_specs=[VMEM] * 5,
        out_specs=[VMEM] * 12,
        compiler_params=params(12),
        name="start",
    )(source, permittivity, src_in, eps_in, frequency.reshape(1, 1))

    def plane(outer, k, p, q, gq, halo, m):
        return pl.pallas_call(
            functools.partial(plane_kernel, outer, k),
            out_shape=[field, pair, pair],
            in_specs=[VMEM] * 9,
            out_specs=[VMEM] * 3,
            compiler_params=params(12),
            cost_estimate=cost(2_000_000),
            name=("outer" if outer else "inner") + str(k),
        )(p, q, gq, halo, m, cy, cz, cx, ct)

    def gram(k, copies, os, ns, row):
        outs = [shape(1, LANES) if copies == 1 else shape(copies, 1, LANES)]
        if k:
            outs.append(shape(2, 3, 2, 2, rows, LANES))
        args = [*os[: k + 1], *ns[: k + 1]] + ([row] if k else [])
        got = pl.pallas_call(
            functools.partial(gram_kernel, k, copies),
            out_shape=outs,
            in_specs=[VMEM] * len(args),
            out_specs=[VMEM] * len(outs),
            compiler_params=params(12),
            cost_estimate=cost(500_000 * (k + 1)),
            name="gram" + str(k),
        )(*args)
        return (got[0], lax.ppermute(got[1], "gy", both)) if k else (got[0], None)

    os, ns, xs = [o], [n], []
    row = None
    for k in range(DEGREE):
        far = lax.ppermute(off, ("gx", "gy"), ring)
        near = lax.ppermute(on, "gy", both)
        row, x = gram(k, 1, os, ns, row)
        if k:
            xs.append(x)
        o2, go2, off = plane(True, k, os[k], ns[k], gn, far, mo)
        n2, gn2, on = plane(False, k, ns[k], os[k], go, near, mn)
        go, gn = go2, gn2
        os.append(o2)
        ns.append(n2)
    row, x = gram(DEGREE, 2 * chips, os, ns, row)
    xs.append(x)
    gathered = lax.all_to_all(row, ("gx", "gy"), split_axis=0, concat_axis=0, tiled=True)
    whole = shape(*source.shape)
    local = pltpu.VMEM(source.shape[1:], F32)
    return tuple(
        pl.pallas_call(
            last_step_kernel,
            out_shape=[whole, whole],
            in_specs=[VMEM] * 21,
            out_specs=[ANY, ANY],
            scratch_shapes=[local, local, pltpu.SemaphoreType.DMA((2, 3))],
            compiler_params=params(16),
            name="combine",
        )(gathered, ct, source, *os[1:], *ns[1:], *xs)
    )


def solution(mesh):
    placed = (P("groups", None, None, "gx", "gy", None), P("groups", "gx", "gy", None), P())
    out = P("groups", None, None, "gx", "gy", None)
    return jax.shard_map(body, mesh=mesh, in_specs=placed, out_specs=(out, out), check_vma=False)
```

time: 428 us -> 97.8 us (0.23)
  between operations: 100 us -> 1.7 us
  other arithmetic: 76.9 us -> 0 us
  waiting for transfers between devices: 89 us -> 16 us
  starting transfers between devices: 105 us -> 50.4 us
  local copies, waits for them, and re-layouts: 36.4 us -> 7.95 us
  Pallas kernels: 0 us -> 21.4 us
  blocking collectives: 17.5 us -> 0 us
    all_to_all x6 -> x1, waiting for transfers between devices: 56.8 us -> 11.6 us  [body(): lax.all_to_all(row, ('gx', 'gy'), split_axis=0, concat_axis=0, tiled=True)]
    sub x77 -> x0, other arithmetic: 38.9 us -> none  [the longest x15 27.6 us: scaled(): real_part = values[:, :, 0] * real_scale - values[:, :, 1] * imag_scale]
    all_to_all x6 -> x1, starting transfers between devices: 40.5 us -> 5.41 us  [body(): lax.all_to_all(row, ('gx', 'gy'), split_axis=0, concat_axis=0, tiled=True)]
    ppermute x24 -> x20, waiting for transfers between devices: 32.1 us -> 4.39 us  [the longest x6 2.35 us: body(): far = lax.ppermute(off, ('gx', 'gy'), ring)]
    pallas_call x0 -> x21, Pallas kernels: none -> 21.4 us  [the longest x7 8.5 us: gram(): pl.pallas_call(functools.partial(gram_kernel, k, copies), out_shape=outs,...]
    ppermute x24 -> x20, starting transfers between devices: 64.3 us -> 45 us  [the longest x6 32.8 us: body(): near = lax.ppermute(on, 'gy', both)]
    all_to_all x1 -> x0, blocking collectives: 17.5 us -> none  [sent_to_all(): return lax.all_to_all(copies, axis, split_axis=0, concat_axis=0, tiled=True)]
    slice x40 -> x0, local copies, waits for them, and re-layouts: 17.2 us -> none  [the longest x4 4.27 us: complex_times(): other[0]]
  transfers between devices with their start and end apart: 30 -> 21, of which waited for: 22 -> 7; matrix products, arithmetic and copies ran while one was open for 3% -> 1% of each run, Pallas kernels for 0% -> 16%
where the time goes in v1:
time: 97.8 us; the launch traced here: 97.4 us
  starting transfers between devices  50.4 us (52%)
  Pallas kernels  21.4 us (22%)
  waiting for transfers between devices  16 us (16%)
  local copies, waits for them, and re-layouts  7.95 us (8%)
  between operations  1.7 us (2%)
    ppermute x6, starting transfers between devices, body(): near = lax.ppermute(on, 'gy', both)  32.8 us
    all_to_all x1, waiting for transfers between devices, body(): lax.all_to_all(row, ('gx', 'gy'), split_axis=0, concat_axis=0, tiled=True)  11.6 us
    ppermute x1, starting transfers between devices, body(): lax.ppermute(lax.dynamic_slice_in_dim(source[0], away, half_x, axis=2), '...  10 us
    pallas_call x7, Pallas kernels, gram(): pl.pallas_call(functools.partial(gram_kernel, k, copies), out_shape=outs,...  8.5 us
    pallas_call x12, Pallas kernels, plane(): pl.pallas_call(functools.partial(plane_kernel, outer, k), out_shape=[fiel...  7.16 us
    unnamed x24, local copies, waits for them, and re-layouts  5.91 us
    all_to_all x1, starting transfers between devices, body(): lax.all_to_all(row, ('gx', 'gy'), split_axis=0, concat_axis=0, tiled=True)  5.41 us
    pallas_call x1, Pallas kernels, body(): pl.pallas_call(last_step_kernel, out_shape=[whole, whole], in_specs=[VMEM...  5.28 us
  transfers between devices with their start and end apart: 21, of which 7 were waited for; matrix products, arithmetic and copies ran while one was open for 1% of the time, Pallas kernels for 16%

profile of v1, /device:TPU:69, one launch (start us, length us, event | category | flops | bytes accessed | tf_op | source)
XLA Modules:
  0.0 97.4 jit_solution(14026585838561832771)
XLA Ops:
  0.6 1.1 %dynamic-slice_bitcast_fusion = f32[3,2,2,32,256]{4,3,2,1,0:T(8,128)S(1)} fusion(f32[1,3,2,4,32,256]{5,4,3,2,1,0:T(8,128)} %refs_2_.1, s32[]{:T(128)S(6)} %select_n.4), kind=kLoop, calls=%fused_computation | loop fusion | bytes 786436 | tf_op jit(solution)/shard_map/dynamic_slice | solution.py:656
  1.8 10.0 %collective-permute-start = (f32[3,2,2,32,256]{4,3,2,1,0:T(8,128)S(1)}, f32[3,2,2,32,256]{4,3,2,1,0:T(8,128)S(1)}, u32[]{:S(2)}, u32[]{:S(2)}) collective-permute-start(f32[3,2,2,32,256]{4,3,2,1,0:T(8,128)S(1)} %dynamic-slice_bitcast_fusion), channel_id=1, source_target_pairs={{0,1},{1,0},{2,3},{3,2},{4,5},{5,4},{6,7},{7,6},{8,9},{9,8},{10,11... | collective-permute-start | bytes 1179656 | tf_op jit(solution)/shard_map/ppermute | solution.py:655
  11.8 0.9 constant_dynamic-slice_fusion
  13.5 0.8 collective-permute-done.1.eps_in
  14.9 4.1 %collective-permute-start.3 = (f32[2,2,2,64,128]{4,3,2,1,0:T(8,128)S(1)}, f32[2,2,2,64,128]{4,3,2,1,0:T(8,128)S(1)}, u32[]{:S(2)}, u32[]{:S(2)}) collective-permute-start(f32[2,2,2,64,128]{4,3,2,1,0:T(8,128)S(1)} %get-tuple-element.69), channel_id=1, source_target_pairs={{0,1},{1,0},{2,3},{3,2},{4,5},{5,4},{6,7},{7,6},{8,9},{9,8},{10,11... | collective-permute-start | bytes 786440 | tf_op jit(solution)/shard_map/ppermute | solution.py:707
  19.0 1.9 %collective-permute-done.2.halo_ref = f32[2,2,2,64,128]{4,3,2,1,0:T(8,128)S(1)} collective-permute-done((f32[2,2,2,64,128]{4,3,2,1,0:T(8,128)S(1)}, f32[2,2,2,64,128]{4,3,2,1,0:T(8,128)S(1)}, u32[]{:S(2)}, u32[]{:S(2)}) %collective-permute-start.2) | collective-permute-done | bytes 262176 | tf_op jit(solution)/shard_map/ppermute | solution.py:706
  20.9 0.5 outer0.1
  21.6 0.5 inner0.1
  22.1 5.1 %collective-permute-start.5 = (f32[2,2,2,64,128]{4,3,2,1,0:T(8,128)S(1)}, f32[2,2,2,64,128]{4,3,2,1,0:T(8,128)S(1)}, u32[]{:S(2)}, u32[]{:S(2)}) collective-permute-start(f32[2,2,2,64,128]{4,3,2,1,0:T(8,128)S(1)} %get-tuple-element.76), channel_id=1, source_target_pairs={{0,1},{1,0},{2,3},{3,2},{4,5},{5,4},{6,7},{7,6},{8,9},{9,8},{10,11... | collective-permute-start | bytes 786440 | tf_op jit(solution)/shard_map/ppermute | solution.py:707
  28.8 5.9 %collective-permute-start.7 = (f32[2,2,2,64,128]{4,3,2,1,0:T(8,128)S(1)}, f32[2,2,2,64,128]{4,3,2,1,0:T(8,128)S(1)}, u32[]{:S(2)}, u32[]{:S(2)}) collective-permute-start(f32[2,2,2,64,128]{4,3,2,1,0:T(8,128)S(1)} %get-tuple-element.82), channel_id=1, source_target_pairs={{0,1},{1,0},{2,3},{3,2},{4,5},{5,4},{6,7},{7,6},{8,9},{9,8},{10,11... | collective-permute-start | bytes 786440 | tf_op jit(solution)/shard_map/ppermute | solution.py:707
  35.4 0.6 collective-permute-done.7.halo_ref
  36.4 5.9 %collective-permute-start.9 = (f32[2,2,2,64,128]{4,3,2,1,0:T(8,128)S(1)}, f32[2,2,2,64,128]{4,3,2,1,0:T(8,128)S(1)}, u32[]{:S(2)}, u32[]{:S(2)}) collective-permute-start(f32[2,2,2,64,128]{4,3,2,1,0:T(8,128)S(1)} %get-tuple-element.88), channel_id=1, source_target_pairs={{0,1},{1,0},{2,3},{3,2},{4,5},{5,4},{6,7},{7,6},{8,9},{9,8},{10,11... | collective-permute-start | bytes 786440 | tf_op jit(solution)/shard_map/ppermute | solution.py:707
  43.0 0.6 collective-permute-done.9.halo_ref
  44.0 6.1 %collective-permute-start.11 = (f32[2,2,2,64,128]{4,3,2,1,0:T(8,128)S(1)}, f32[2,2,2,64,128]{4,3,2,1,0:T(8,128)S(1)}, u32[]{:S(2)}, u32[]{:S(2)}) collective-permute-start(f32[2,2,2,64,128]{4,3,2,1,0:T(8,128)S(1)} %get-tuple-element.94), channel_id=1, source_target_pairs={{0,1},{1,0},{2,3},{3,2},{4,5},{5,4},{6,7},{7,6},{8,9},{9,8},{10,11... | collective-permute-start | bytes 786440 | tf_op jit(solution)/shard_map/ppermute | solution.py:707
  52.0 5.5 %collective-permute-start.13 = (f32[2,2,2,64,128]{4,3,2,1,0:T(8,128)S(1)}, f32[2,2,2,64,128]{4,3,2,1,0:T(8,128)S(1)}, u32[]{:S(2)}, u32[]{:S(2)}) collective-permute-start(f32[2,2,2,64,128]{4,3,2,1,0:T(8,128)S(1)} %get-tuple-element.100), channel_id=1, source_target_pairs={{0,1},{1,0},{2,3},{3,2},{4,5},{5,4},{6,7},{7,6},{8,9},{9,8},{10,11... | collective-permute-start | bytes 786440 | tf_op jit(solution)/shard_map/ppermute | solution.py:707
  57.5 1.2 %gram2.1 = (f32[1,128]{1,0:T(1,128)S(1)}, f32[2,3,2,2,32,128]{5,4,3,2,1,0:T(8,128)}) custom-call(f32[3,2,2,64,128]{4,3,2,1,0:T(8,128)S(1)} %get-tuple-element.58.p_ref.q_ref.refs_0_, f32[3,2,2,64,128]{4,3,2,1,0:T(8,128)S(1)} %get-tuple-element.67.p_ref.q_ref.refs_1_.refs_3_, f32[3,2,2,64,128]{4,3,2,1,0:T(8,128)S(1)} %get-tuple-element.74.p_ref.q_ref.refs_2_.refs_4_, ...), custom_call_target="tpu_custom_call" | custom-call | flops 1500000 | tf_op jit(solution)/shard_map/gram2/pallas_call | solution.py:692
  58.8 1.4 %gram3.1 = (f32[1,128]{1,0:T(1,128)S(1)}, f32[2,3,2,2,32,128]{5,4,3,2,1,0:T(8,128)}) custom-call(f32[3,2,2,64,128]{4,3,2,1,0:T(8,128)S(1)} %get-tuple-element.58.p_ref.q_ref.refs_0_, f32[3,2,2,64,128]{4,3,2,1,0:T(8,128)S(1)} %get-tuple-element.67.p_ref.q_ref.refs_1_.refs_3_, f32[3,2,2,64,128]{4,3,2,1,0:T(8,128)S(1)} %get-tuple-element.74.p_ref.q_ref.refs_2_.refs_4_, ...), custom_call_target="tpu_custom_call" | custom-call | flops 2000000 | tf_op jit(solution)/shard_map/gram3/pallas_call | solution.py:692
  60.2 0.5 collective-permute-start.16
  60.7 1.5 %gram4.1 = (f32[1,128]{1,0:T(1,128)S(1)}, f32[2,3,2,2,32,128]{5,4,3,2,1,0:T(8,128)}) custom-call(f32[3,2,2,64,128]{4,3,2,1,0:T(8,128)S(1)} %get-tuple-element.58.p_ref.q_ref.refs_0_, f32[3,2,2,64,128]{4,3,2,1,0:T(8,128)S(1)} %get-tuple-element.67.p_ref.q_ref.refs_1_.refs_3_, f32[3,2,2,64,128]{4,3,2,1,0:T(8,128)S(1)} %get-tuple-element.74.p_ref.q_ref.refs_2_.refs_4_, ...), custom_call_target="tpu_custom_call" | custom-call | flops 2500000 | tf_op jit(solution)/shard_map/gram4/pallas_call | solution.py:692
  62.2 1.7 %gram5.1 = (f32[1,128]{1,0:T(1,128)S(1)}, f32[2,3,2,2,32,128]{5,4,3,2,1,0:T(8,128)}) custom-call(f32[3,2,2,64,128]{4,3,2,1,0:T(8,128)S(1)} %get-tuple-element.58.p_ref.q_ref.refs_0_, f32[3,2,2,64,128]{4,3,2,1,0:T(8,128)S(1)} %get-tuple-element.67.p_ref.q_ref.refs_1_.refs_3_, f32[3,2,2,64,128]{4,3,2,1,0:T(8,128)S(1)} %get-tuple-element.74.p_ref.q_ref.refs_2_.refs_4_, ...), custom_call_target="tpu_custom_call" | custom-call | flops 3000000 | tf_op jit(solution)/shard_map/gram5/pallas_call | solution.py:692
  64.0 1.3 %outer5.1 = (f32[3,2,2,64,128]{4,3,2,1,0:T(8,128)S(1)}, f32[2,2,2,64,128]{4,3,2,1,0:T(8,128)}, f32[2,2,2,64,128]{4,3,2,1,0:T(8,128)}) custom-call(f32[3,2,2,64,128]{4,3,2,1,0:T(8,128)S(1)} %get-tuple-element.92.p_ref.q_ref.refs_5_.refs_7_, f32[3,2,2,64,128]{4,3,2,1,0:T(8,128)S(1)} %get-tuple-element.95.q_ref.p_ref.refs_11_.refs_12_.refs_13_, ...), custom_call_target="tpu_custom_call" | custom-call | flops 2000000 | tf_op jit(solution)/shard_map/outer5/pallas_call | solution.py:677
  65.7 1.2 %inner5.1 = (f32[3,2,2,64,128]{4,3,2,1,0:T(8,128)S(1)}, f32[2,2,2,64,128]{4,3,2,1,0:T(8,128)}, f32[2,2,2,64,128]{4,3,2,1,0:T(8,128)}) custom-call(f32[3,2,2,64,128]{4,3,2,1,0:T(8,128)S(1)} %get-tuple-element.95.q_ref.p_ref.refs_11_.refs_12_.refs_13_, f32[3,2,2,64,128]{4,3,2,1,0:T(8,128)S(1)} %get-tuple-element.92.p_ref.q_ref.refs_5_.refs_7_, ...), custom_call_target="tpu_custom_call" | custom-call | flops 2000000 | tf_op jit(solution)/shard_map/inner5/pallas_call | solution.py:677
  67.0 2.0 %gram6.1 = (f32[32,1,128]{2,1,0:T(1,128)S(1)}, f32[2,3,2,2,32,128]{5,4,3,2,1,0:T(8,128)}) custom-call(f32[3,2,2,64,128]{4,3,2,1,0:T(8,128)S(1)} %get-tuple-element.58.p_ref.q_ref.refs_0_, f32[3,2,2,64,128]{4,3,2,1,0:T(8,128)S(1)} %get-tuple-element.67.p_ref.q_ref.refs_1_.refs_3_, f32[3,2,2,64,128]{4,3,2,1,0:T(8,128)S(1)} %get-tuple-element.74.p_ref.q_ref.refs_2_.refs_4_, ...), custom_call_target="tpu_custom_call" | custom-call | flops 3500000 | tf_op jit(solution)/shard_map/gram6/pallas_call | solution.py:692
  68.9 0.8 copy-done.9
  69.8 5.4 %all-to-all-start = ((f32[32,1,128]{2,1,0:T(1,128)}), f32[32,1,128]{2,1,0:T(1,128)}, u32[]{:S(2)}, u32[]{:S(2)}) async-start(f32[32,1,128]{2,1,0:T(1,128)} %copy-done.11), calls=%async_computation | async-start | bytes 32768 | tf_op jit(solution)/shard_map/all_to_all | solution.py:718
  75.2 11.6 %all-to-all-done.refs_0_ = f32[32,1,128]{2,1,0:T(1,128)} async-done(((f32[32,1,128]{2,1,0:T(1,128)}), f32[32,1,128]{2,1,0:T(1,128)}, u32[]{:S(2)}, u32[]{:S(2)}) %all-to-all-start) | async-done | bytes 16416 | tf_op jit(solution)/shard_map/all_to_all | solution.py:718
  86.8 1.0 %copy-done.1 = f32[3,2,2,64,128]{4,3,2,1,0:T(8,128)S(1)} copy-done((f32[3,2,2,64,128]{4,3,2,1,0:T(8,128)S(1)}, f32[3,2,2,64,128]{4,3,2,1,0:T(8,128)}, u32[]{:S(2)}) %copy-start.1) | copy-done | bytes 393240
  87.8 1.1 %copy-done.3 = f32[1,3,2,4,32,256]{5,4,3,2,1,0:T(8,128)S(1)} copy-done((f32[1,3,2,4,32,256]{5,4,3,2,1,0:T(8,128)S(1)}, f32[1,3,2,4,32,256]{5,4,3,2,1,0:T(8,128)}, u32[]{:S(2)}) %copy-start.3) | copy-done | bytes 786456
  89.0 1.0 %copy-done.5 = f32[3,2,2,64,128]{4,3,2,1,0:T(8,128)S(1)} copy-done((f32[3,2,2,64,128]{4,3,2,1,0:T(8,128)S(1)}, f32[3,2,2,64,128]{4,3,2,1,0:T(8,128)}, u32[]{:S(2)}) %copy-start.5) | copy-done | bytes 393240
  90.0 1.0 %copy-done.7 = f32[3,2,2,64,128]{4,3,2,1,0:T(8,128)S(1)} copy-done((f32[3,2,2,64,128]{4,3,2,1,0:T(8,128)S(1)}, f32[3,2,2,64,128]{4,3,2,1,0:T(8,128)}, u32[]{:S(2)}) %copy-start.7) | copy-done | bytes 393240
  91.0 1.0 %copy-done.10 = f32[2,3,2,2,32,128]{5,4,3,2,1,0:T(8,128)S(1)} copy-done((f32[2,3,2,2,32,128]{5,4,3,2,1,0:T(8,128)S(1)}, f32[2,3,2,2,32,128]{5,4,3,2,1,0:T(8,128)}, u32[]{:S(2)}) %copy-start.10) | copy-done | bytes 393240
  91.9 5.3 %combine.1 = (f32[1,3,2,4,32,256]{5,4,3,2,1,0:T(8,128)}, f32[1,3,2,4,32,256]{5,4,3,2,1,0:T(8,128)}) custom-call(f32[32,1,128]{2,1,0:T(1,128)} %all-to-all-done.refs_0_, f32[8,128]{1,0:T(8,128)S(1)} %get-tuple-element.66.ct_ref.refs_1_, f32[1,3,2,4,32,256]{5,4,3,2,1,0:T(8,128)S(1)} %copy-done.3, ...), custom_call_target="tpu_custom_call" | custom-call | tf_op jit(solution)/shard_map/combine/pallas_call | solution.py:722
  (57 shorter events, 7.0 us)
Async XLA Ops:
  0.6 13.7 %copy-start.2 = (f32[1,3,2,4,32,256]{5,4,3,2,1,0:T(8,128)S(1)}, f32[1,3,2,4,32,256]{5,4,3,2,1,0:T(8,128)}, u32[]{:S(2)}) copy-start(f32[1,3,2,4,32,256]{5,4,3,2,1,0:T(8,128)} %refs_2_.1) | copy-start | bytes 2359300
  1.7 12.5 %copy-start.8 = (f32[3,4,32,256]{3,2,1,0:T(8,128)S(1)}, f32[3,4,32,256]{3,2,1,0:T(8,128)}, u32[]{:S(2)}) copy-start(f32[3,4,32,256]{3,2,1,0:T(8,128)} %eps.1) | copy-start | bytes 1179652
  1.8 12.5 %collective-permute-start = (f32[3,2,2,32,256]{4,3,2,1,0:T(8,128)S(1)}, f32[3,2,2,32,256]{4,3,2,1,0:T(8,128)S(1)}, u32[]{:S(2)}, u32[]{:S(2)}) collective-permute-start(f32[3,2,2,32,256]{4,3,2,1,0:T(8,128)S(1)} %dynamic-slice_bitcast_fusion), channel_id=1, source_target_pairs={{0,1},{1,0},{2,3},{3,2},{4,5},{5,4},{6,7},{7,6},{8,9},{9,8},{10,11... | collective-permute-start | bytes 1179656 | tf_op jit(solution)/shard_map/ppermute | solution.py:655
  12.7 1.6 %collective-permute-start.1 = (f32[3,2,32,256]{3,2,1,0:T(8,128)S(1)}, f32[3,2,32,256]{3,2,1,0:T(8,128)S(1)}, u32[]{:S(2)}, u32[]{:S(2)}) collective-permute-start(f32[3,2,32,256]{3,2,1,0:T(8,128)S(1)} %constant_dynamic-slice_fusion), channel_id=1, source_target_pairs={{0,1},{1,0},{2,3},{3,2},{4,5},{5,4},{6,7},{7,6},{8,9},{9,8},{10,11... | collective-permute-start | bytes 589832 | tf_op jit(solution)/shard_map/ppermute | solution.py:658
  14.7 6.2 %collective-permute-start.2 = (f32[2,2,2,64,128]{4,3,2,1,0:T(8,128)S(1)}, f32[2,2,2,64,128]{4,3,2,1,0:T(8,128)S(1)}, u32[]{:S(2)}, u32[]{:S(2)}) collective-permute-start(f32[2,2,2,64,128]{4,3,2,1,0:T(8,128)S(1)} %get-tuple-element.61), channel_id=1, source_target_pairs={{1,2},{3,4},{5,6},{7,8},{9,10},{11,12},{13,14},{15,16},{17,18},{19... | collective-permute-start | bytes 786440 | tf_op jit(solution)/shard_map/ppermute | solution.py:706
  14.9 6.7 %collective-permute-start.3 = (f32[2,2,2,64,128]{4,3,2,1,0:T(8,128)S(1)}, f32[2,2,2,64,128]{4,3,2,1,0:T(8,128)S(1)}, u32[]{:S(2)}, u32[]{:S(2)}) collective-permute-start(f32[2,2,2,64,128]{4,3,2,1,0:T(8,128)S(1)} %get-tuple-element.69), channel_id=1, source_target_pairs={{0,1},{1,0},{2,3},{3,2},{4,5},{5,4},{6,7},{7,6},{8,9},{9,8},{10,11... | collective-permute-start | bytes 786440 | tf_op jit(solution)/shard_map/ppermute | solution.py:707
  21.4 6.2 %collective-permute-start.4 = (f32[2,2,2,64,128]{4,3,2,1,0:T(8,128)S(1)}, f32[2,2,2,64,128]{4,3,2,1,0:T(8,128)S(1)}, u32[]{:S(2)}, u32[]{:S(2)}) collective-permute-start(f32[2,2,2,64,128]{4,3,2,1,0:T(8,128)S(1)} %get-tuple-element.73), channel_id=1, source_target_pairs={{1,2},{3,4},{5,6},{7,8},{9,10},{11,12},{13,14},{15,16},{17,18},{19... | collective-permute-start | bytes 786440 | tf_op jit(solution)/shard_map/ppermute | solution.py:706
  22.1 6.3 %collective-permute-start.5 = (f32[2,2,2,64,128]{4,3,2,1,0:T(8,128)S(1)}, f32[2,2,2,64,128]{4,3,2,1,0:T(8,128)S(1)}, u32[]{:S(2)}, u32[]{:S(2)}) collective-permute-start(f32[2,2,2,64,128]{4,3,2,1,0:T(8,128)S(1)} %get-tuple-element.76), channel_id=1, source_target_pairs={{0,1},{1,0},{2,3},{3,2},{4,5},{5,4},{6,7},{7,6},{8,9},{9,8},{10,11... | collective-permute-start | bytes 786440 | tf_op jit(solution)/shard_map/ppermute | solution.py:707
  28.1 6.7 %collective-permute-start.6 = (f32[2,2,2,64,128]{4,3,2,1,0:T(8,128)S(1)}, f32[2,2,2,64,128]{4,3,2,1,0:T(8,128)S(1)}, u32[]{:S(2)}, u32[]{:S(2)}) collective-permute-start(f32[2,2,2,64,128]{4,3,2,1,0:T(8,128)S(1)} %get-tuple-element.79), channel_id=1, source_target_pairs={{1,2},{3,4},{5,6},{7,8},{9,10},{11,12},{13,14},{15,16},{17,18},{19... | collective-permute-start | bytes 786440 | tf_op jit(solution)/shard_map/ppermute | solution.py:706
  28.8 7.1 %collective-permute-start.7 = (f32[2,2,2,64,128]{4,3,2,1,0:T(8,128)S(1)}, f32[2,2,2,64,128]{4,3,2,1,0:T(8,128)S(1)}, u32[]{:S(2)}, u32[]{:S(2)}) collective-permute-start(f32[2,2,2,64,128]{4,3,2,1,0:T(8,128)S(1)} %get-tuple-element.82), channel_id=1, source_target_pairs={{0,1},{1,0},{2,3},{3,2},{4,5},{5,4},{6,7},{7,6},{8,9},{9,8},{10,11... | collective-permute-start | bytes 786440 | tf_op jit(solution)/shard_map/ppermute | solution.py:707
  35.2 7.1 %collective-permute-start.8 = (f32[2,2,2,64,128]{4,3,2,1,0:T(8,128)S(1)}, f32[2,2,2,64,128]{4,3,2,1,0:T(8,128)S(1)}, u32[]{:S(2)}, u32[]{:S(2)}) collective-permute-start(f32[2,2,2,64,128]{4,3,2,1,0:T(8,128)S(1)} %get-tuple-element.85), channel_id=1, source_target_pairs={{1,2},{3,4},{5,6},{7,8},{9,10},{11,12},{13,14},{15,16},{17,18},{19... | collective-permute-start | bytes 786440 | tf_op jit(solution)/shard_map/ppermute | solution.py:706
  36.4 7.1 %collective-permute-start.9 = (f32[2,2,2,64,128]{4,3,2,1,0:T(8,128)S(1)}, f32[2,2,2,64,128]{4,3,2,1,0:T(8,128)S(1)}, u32[]{:S(2)}, u32[]{:S(2)}) collective-permute-start(f32[2,2,2,64,128]{4,3,2,1,0:T(8,128)S(1)} %get-tuple-element.88), channel_id=1, source_target_pairs={{0,1},{1,0},{2,3},{3,2},{4,5},{5,4},{6,7},{7,6},{8,9},{9,8},{10,11... | collective-permute-start | bytes 786440 | tf_op jit(solution)/shard_map/ppermute | solution.py:707
  42.8 8.1 %collective-permute-start.10 = (f32[2,2,2,64,128]{4,3,2,1,0:T(8,128)S(1)}, f32[2,2,2,64,128]{4,3,2,1,0:T(8,128)S(1)}, u32[]{:S(2)}, u32[]{:S(2)}) collective-permute-start(f32[2,2,2,64,128]{4,3,2,1,0:T(8,128)S(1)} %get-tuple-element.91), channel_id=1, source_target_pairs={{1,2},{3,4},{5,6},{7,8},{9,10},{11,12},{13,14},{15,16},{17,18},{19... | collective-permute-start | bytes 786440 | tf_op jit(solution)/shard_map/ppermute | solution.py:706
  44.0 7.5 %collective-permute-start.11 = (f32[2,2,2,64,128]{4,3,2,1,0:T(8,128)S(1)}, f32[2,2,2,64,128]{4,3,2,1,0:T(8,128)S(1)}, u32[]{:S(2)}, u32[]{:S(2)}) collective-permute-start(f32[2,2,2,64,128]{4,3,2,1,0:T(8,128)S(1)} %get-tuple-element.94), channel_id=1, source_target_pairs={{0,1},{1,0},{2,3},{3,2},{4,5},{5,4},{6,7},{7,6},{8,9},{9,8},{10,11... | collective-permute-start | bytes 786440 | tf_op jit(solution)/shard_map/ppermute | solution.py:707
  50.8 18.2 %collective-permute-start.14 = (f32[2,3,2,2,32,128]{5,4,3,2,1,0:T(8,128)S(1)}, f32[2,3,2,2,32,128]{5,4,3,2,1,0:T(8,128)S(1)}, u32[]{:S(2)}, u32[]{:S(2)}) collective-permute-start(f32[2,3,2,2,32,128]{5,4,3,2,1,0:T(8,128)S(1)} %get-tuple-element.108), channel_id=1, source_target_pairs={{0,1},{1,0},{2,3},{3,2},{4,5},{5,4},{6,7},{7,6},{8,9},{9,8},{10,11... | collective-permute-start | bytes 1179656 | tf_op jit(solution)/shard_map/ppermute | solution.py:701
  51.4 12.6 %collective-permute-start.12 = (f32[2,2,2,64,128]{4,3,2,1,0:T(8,128)S(1)}, f32[2,2,2,64,128]{4,3,2,1,0:T(8,128)S(1)}, u32[]{:S(2)}, u32[]{:S(2)}) collective-permute-start(f32[2,2,2,64,128]{4,3,2,1,0:T(8,128)S(1)} %get-tuple-element.97), channel_id=1, source_target_pairs={{1,2},{3,4},{5,6},{7,8},{9,10},{11,12},{13,14},{15,16},{17,18},{19... | collective-permute-start | bytes 786440 | tf_op jit(solution)/shard_map/ppermute | solution.py:706
  52.0 15.0 %copy-start = (f32[3,2,2,64,128]{4,3,2,1,0:T(8,128)}, f32[3,2,2,64,128]{4,3,2,1,0:T(8,128)S(1)}, u32[]{:S(2)}) copy-start(f32[3,2,2,64,128]{4,3,2,1,0:T(8,128)S(1)} %get-tuple-element.95.q_ref.p_ref.refs_11_.refs_12_.refs_13_) | copy-start | bytes 1179652
  52.0 13.2 %collective-permute-start.13 = (f32[2,2,2,64,128]{4,3,2,1,0:T(8,128)S(1)}, f32[2,2,2,64,128]{4,3,2,1,0:T(8,128)S(1)}, u32[]{:S(2)}, u32[]{:S(2)}) collective-permute-start(f32[2,2,2,64,128]{4,3,2,1,0:T(8,128)S(1)} %get-tuple-element.100), channel_id=1, source_target_pairs={{0,1},{1,0},{2,3},{3,2},{4,5},{5,4},{6,7},{7,6},{8,9},{9,8},{10,11... | collective-permute-start | bytes 786440 | tf_op jit(solution)/shard_map/ppermute | solution.py:707
  58.8 16.4 %collective-permute-start.15 = (f32[2,3,2,2,32,128]{5,4,3,2,1,0:T(8,128)}, f32[2,3,2,2,32,128]{5,4,3,2,1,0:T(8,128)}, u32[]{:S(2)}, u32[]{:S(2)}) collective-permute-start(f32[2,3,2,2,32,128]{5,4,3,2,1,0:T(8,128)} %get-tuple-element.109), channel_id=1, source_target_pairs={{0,1},{1,0},{2,3},{3,2},{4,5},{5,4},{6,7},{7,6},{8,9},{9,8},{10,11... | collective-permute-start | bytes 1179656 | tf_op jit(solution)/shard_map/ppermute | solution.py:701
  60.2 15.0 %collective-permute-start.16 = (f32[2,3,2,2,32,128]{5,4,3,2,1,0:T(8,128)}, f32[2,3,2,2,32,128]{5,4,3,2,1,0:T(8,128)}, u32[]{:S(2)}, u32[]{:S(2)}) collective-permute-start(f32[2,3,2,2,32,128]{5,4,3,2,1,0:T(8,128)} %get-tuple-element.110), channel_id=1, source_target_pairs={{0,1},{1,0},{2,3},{3,2},{4,5},{5,4},{6,7},{7,6},{8,9},{9,8},{10,11... | collective-permute-start | bytes 1179656 | tf_op jit(solution)/shard_map/ppermute | solution.py:701
  63.9 11.3 %collective-permute-start.17 = (f32[2,3,2,2,32,128]{5,4,3,2,1,0:T(8,128)}, f32[2,3,2,2,32,128]{5,4,3,2,1,0:T(8,128)}, u32[]{:S(2)}, u32[]{:S(2)}) collective-permute-start(f32[2,3,2,2,32,128]{5,4,3,2,1,0:T(8,128)} %get-tuple-element.111), channel_id=1, source_target_pairs={{0,1},{1,0},{2,3},{3,2},{4,5},{5,4},{6,7},{7,6},{8,9},{9,8},{10,11... | collective-permute-start | bytes 1179656 | tf_op jit(solution)/shard_map/ppermute | solution.py:701
  65.2 1.7 %copy-start.4 = (f32[3,2,2,64,128]{4,3,2,1,0:T(8,128)}, f32[3,2,2,64,128]{4,3,2,1,0:T(8,128)S(1)}, u32[]{:S(2)}) copy-start(f32[3,2,2,64,128]{4,3,2,1,0:T(8,128)S(1)} %get-tuple-element.98.refs_6_.refs_8_) | copy-start | bytes 1179652
  65.2 21.6 %collective-permute-start.18 = (f32[2,3,2,2,32,128]{5,4,3,2,1,0:T(8,128)}, f32[2,3,2,2,32,128]{5,4,3,2,1,0:T(8,128)}, u32[]{:S(2)}, u32[]{:S(2)}) collective-permute-start(f32[2,3,2,2,32,128]{5,4,3,2,1,0:T(8,128)} %get-tuple-element.112), channel_id=1, source_target_pairs={{0,1},{1,0},{2,3},{3,2},{4,5},{5,4},{6,7},{7,6},{8,9},{9,8},{10,11... | collective-permute-start | bytes 1179656 | tf_op jit(solution)/shard_map/ppermute | solution.py:701
  67.0 2.0 %copy-start.6 = (f32[3,2,2,64,128]{4,3,2,1,0:T(8,128)}, f32[3,2,2,64,128]{4,3,2,1,0:T(8,128)S(1)}, u32[]{:S(2)}) copy-start(f32[3,2,2,64,128]{4,3,2,1,0:T(8,128)S(1)} %get-tuple-element.101.refs_13_.refs_14_) | copy-start | bytes 1179652
  68.9 0.8 copy-start.11
  69.7 17.1 %collective-permute-start.19 = (f32[2,3,2,2,32,128]{5,4,3,2,1,0:T(8,128)}, f32[2,3,2,2,32,128]{5,4,3,2,1,0:T(8,128)}, u32[]{:S(2)}, u32[]{:S(2)}) collective-permute-start(f32[2,3,2,2,32,128]{5,4,3,2,1,0:T(8,128)} %get-tuple-element.113), channel_id=1, source_target_pairs={{0,1},{1,0},{2,3},{3,2},{4,5},{5,4},{6,7},{7,6},{8,9},{9,8},{10,11... | collective-permute-start | bytes 1179656 | tf_op jit(solution)/shard_map/ppermute | solution.py:701
  69.8 17.1 %all-to-all-start = ((f32[32,1,128]{2,1,0:T(1,128)}), f32[32,1,128]{2,1,0:T(1,128)}, u32[]{:S(2)}, u32[]{:S(2)}) async-start(f32[32,1,128]{2,1,0:T(1,128)} %copy-done.11), calls=%async_computation | async-start | bytes 32768 | tf_op jit(solution)/shard_map/all_to_all | solution.py:718
  86.8 1.0 %copy-start.1 = (f32[3,2,2,64,128]{4,3,2,1,0:T(8,128)S(1)}, f32[3,2,2,64,128]{4,3,2,1,0:T(8,128)}, u32[]{:S(2)}) copy-start(f32[3,2,2,64,128]{4,3,2,1,0:T(8,128)} %copy-done) | copy-start | bytes 1179652
  87.8 1.1 %copy-start.3 = (f32[1,3,2,4,32,256]{5,4,3,2,1,0:T(8,128)S(1)}, f32[1,3,2,4,32,256]{5,4,3,2,1,0:T(8,128)}, u32[]{:S(2)}) copy-start(f32[1,3,2,4,32,256]{5,4,3,2,1,0:T(8,128)} %refs_2_.1) | copy-start | bytes 2359300
  89.0 1.0 %copy-start.5 = (f32[3,2,2,64,128]{4,3,2,1,0:T(8,128)S(1)}, f32[3,2,2,64,128]{4,3,2,1,0:T(8,128)}, u32[]{:S(2)}) copy-start(f32[3,2,2,64,128]{4,3,2,1,0:T(8,128)} %copy-done.4) | copy-start | bytes 1179652
  90.0 1.0 %copy-start.7 = (f32[3,2,2,64,128]{4,3,2,1,0:T(8,128)S(1)}, f32[3,2,2,64,128]{4,3,2,1,0:T(8,128)}, u32[]{:S(2)}) copy-start(f32[3,2,2,64,128]{4,3,2,1,0:T(8,128)} %copy-done.6) | copy-start | bytes 1179652
  91.0 1.0 %copy-start.10 = (f32[2,3,2,2,32,128]{5,4,3,2,1,0:T(8,128)S(1)}, f32[2,3,2,2,32,128]{5,4,3,2,1,0:T(8,128)}, u32[]{:S(2)}) copy-start(f32[2,3,2,2,32,128]{5,4,3,2,1,0:T(8,128)} %copy-done.9) | copy-start | bytes 1179652
  (1 other events, 0.8 us)

commit v2 on v1

--- a/solution.py
+++ b/solution.py
@@ -13,15 +13,17 @@
 pml_strength = 2.0
 LANES = 128
 TILE = 8
+COMBINE_MIB = 12
 
 NODES = (0.0, -1.0, 1.0, 0.577, -0.671, 0.319)
 F32 = jnp.float32
 VMEM = pl.BlockSpec(memory_space=pltpu.VMEM)
 ANY = pl.BlockSpec(memory_space=pl.ANY)
+HBM = pl.BlockSpec(memory_space=pltpu.HBM)
 
 
 def params(mib):
-    return pltpu.CompilerParams(vmem_limit_bytes=mib * 2**20)
+    return pltpu.CompilerParams(vmem_limit_bytes=int(mib * 2**20))
 
 
 def stretch(points, length, frequency):
@@ -145,13 +147,27 @@
     return write
 
 
+def split_kernel(count, s_hbm, e_hbm, *refs):
+    core = lax.axis_index("gy")
+    sems = refs[4]
+    copies = []
+    for n, whose in enumerate((1 - core, core)):
+        at = pl.ds(count * whose, count)
+        copies.append(pltpu.make_async_copy(s_hbm.at[0, :, :, at], refs[2 * n], sems.at[2 * n]))
+        copies.append(pltpu.make_async_copy(e_hbm.at[:, at], refs[2 * n + 1], sems.at[2 * n + 1]))
+    for copy in copies:
+        copy.start()
+    for copy in copies:
+        copy.wait()
+
+
 def start_kernel(
     cells_x, src, eps, src_in, eps_in, freq,
     o_ref, n_ref, mo_ref, mn_ref, go_ref, gn_ref, off_ref, on_ref, cy_ref, cz_ref, cx_ref, ct_ref,
 ):
     core = lax.axis_index("gy")
     chip = lax.axis_index("gx")
-    rows, cols = src.shape[4], src.shape[5]
+    rows, cols = src.shape[3], src.shape[4]
     ny, nx = 2 * rows, cells_x * lax.axis_size("gx")
     half_x = cells_x // 2
     tiles = ny // TILE
@@ -166,10 +182,10 @@
                 z = slice(h * LANES, (h + 1) * LANES)
                 for c in range(3):
                     for part in range(2):
-                        dest[c, part, h, own_rows, :] = src[0, c, part, half_x * first_own + plane, :, z]
+                        dest[c, part, h, own_rows, :] = src[c, part, plane, :, z]
                         dest[c, part, h, other_rows, :] = src_in[c, part, plane, :, z]
                     scale = square[0:1, :]
-                    mdest[c, h, own_rows, :] = eps[c, half_x * first_own + plane, :, z] * scale
+                    mdest[c, h, own_rows, :] = eps[c, plane, :, z] * scale
                     mdest[c, h, other_rows, :] = eps_in[c, plane, :, z] * scale
 
     @pl.when(core == 0)
@@ -226,10 +242,14 @@
         on_ref[...] = n_ref[1:3]
 
 
-def plane_kernel(
-    outer, k, p_ref, q_ref, gq_ref, halo_ref, m_ref, cy_ref, cz_ref, cx_ref, ct_ref,
-    new_ref, g_ref, out_ref,
-):
+def plane_kernel(outer, k, *refs):
+    refs = list(refs)
+    p_ref, q_ref, gq_ref, halo_ref, m_ref, cy_ref, cz_ref, cx_ref, ct_ref = refs[:9]
+    refs = refs[9:]
+    last = k + 1 == DEGREE
+    new_ref = refs[0]
+    g_ref, out_ref = (None, None) if last else refs[1:]
+    give_ref = refs[1] if last else None
     core = lax.axis_index("gy")
     chip = lax.axis_index("gx")
     tiles = p_ref.shape[3] // TILE
@@ -254,17 +274,21 @@
         at_edge = (chip == 0) if edge else (chip == lax.axis_size("gx") - 1)
         closed = jnp.zeros((TILE, LANES), jnp.int32) + at_edge.astype(jnp.int32) > 0
         read_p = tile_reader(p_ref)
-        read_g = tile_reader(halo_ref if left else gq_ref, 2)
+        halo_reader = tile_reader(halo_ref, 2)
+        read_g = halo_reader if left else tile_reader(gq_ref, 2)
         if left:
             read_r = lambda t: tile_reader(q_ref)(t)[1:]
         else:
-            read_r = tile_reader(halo_ref, 2)
+            read_r = halo_reader
         rolled_h = None
         pending = None
         nxt = read_p(0)
         rolled = [[[line.up(nxt[c][h][i]) for i in range(2)] for h in range(2)] for c in (0, 2)]
-        write_new, write_g, write_out = tile_writer(new_ref), tile_writer(g_ref), tile_writer(out_ref)
-        write_edge = write_g if left else write_out
+        write_new = tile_writer(new_ref)
+        if not last:
+            write_g = tile_writer(g_ref)
+            write_out = tile_writer(out_ref)
+            write_edge = write_g if left else write_out
 
         def finish(pend, after):
             t0, ex, rolled_ex, base = pend
@@ -343,9 +367,11 @@
                     made[c].append([(curl[i] - shifted * field[h][i]) * scale for i in range(2)])
                     for i in range(2):
                         write_new(c, i, h, t, made[c][h][i])
-                        if left and c:
+                        if left and c and not last:
                             write_out(c - 1, i, h, t, made[c][h][i])
             rolled_h = new_rolled
+            if last:
+                continue
             dz = z_steps(line, made[0])
             up = [[line.up(made[0][h][i]) for i in range(2)] for h in range(2)]
             base = []
@@ -358,7 +384,12 @@
             if pending is not None:
                 finish(pending, up)
             pending = (t, made[0], up, base)
-        finish(pending, None)
+        if not last:
+            finish(pending, None)
+        else:
+            half = tiles * TILE // 2
+            rows = slice(half, 2 * half) if left == outer else slice(0, half)
+            give_ref[...] = new_ref[:, :, :, rows, :]
 
     left_here = (core == 0) if outer else (core != 0)
 
@@ -391,9 +422,27 @@
     os, ns = refs[:count], refs[count : 2 * count]
     rest = list(refs[2 * count :])
     row_in = rest.pop(0) if k else None
+    store = 0 < k < DEGREE
+    if store and k > 1:
+        rest = rest[2:]
     row_ref = rest.pop(0)
     core = lax.axis_index("gy")
-    tiles = os[0].shape[3] // TILE
+    rows = os[0].shape[3]
+    half = rows // 2
+    pending = []
+    if store:
+        own_ref, give_ref, sems = rest
+        for to, (ref, whose) in enumerate(((own_ref, core), (give_ref, 1 - core))):
+            part = pl.ds(pl.multiple_of(half * whose, TILE), half)
+            for n, source in enumerate((os[k], ns[k])):
+                pending.append(
+                    pltpu.make_async_copy(
+                        source.at[:, :, :, part], ref.at[k - 1, n], sems.at[to, n]
+                    )
+                )
+    for copy in pending:
+        copy.start()
+    tiles = rows // TILE
     zero = jnp.zeros((TILE, LANES), F32)
     real = [[zero, zero] for _ in range(count)]
     imag = [[zero, zero] for _ in range(count)]
@@ -423,15 +472,8 @@
     else:
         for d in range(copies):
             row_ref[d] = row
-    if k:
-        other_ref = rest.pop(0)
-        half = other_ref.shape[4]
-        first = pl.multiple_of(half * (1 - core), TILE)
-        for which, group in enumerate((os, ns)):
-            for c in range(3):
-                for part in range(2):
-                    for h in range(2):
-                        other_ref[which, c, part, h] = group[k][c, part, h, pl.ds(first, half), :]
+    for copy in pending:
+        copy.wait()
 
 
 def quick(a, b):
@@ -585,11 +627,43 @@
 
 
 def last_step_kernel(*refs):
-    gathered, ct_ref, src = refs[:3]
-    os, ns, xs = refs[3:9], refs[9:15], refs[15:21]
-    x_hbm, r_hbm, x_ref, r_ref, sems = refs[21:]
+    gathered, ct_ref, src, own_ref, got_ref, o_last, n_last, o_got, n_got = refs[:9]
+    x_hbm, r_hbm, v0_ref, v_ref, x_ref, r_ref, first_sems, in_sems, sems = refs[9:]
     core = lax.axis_index("gy")
-    half = src.shape[4]
+    half = v_ref.shape[5]
+    coming = [[] for _ in range(3)]
+    for c in range(3):
+        coming[c].append(pltpu.make_async_copy(src.at[0, c], v0_ref.at[c], first_sems.at[c]))
+        for n, (ref, plane) in enumerate(
+            (
+                (own_ref.at[:, 0], 3 * core),
+                (own_ref.at[:, 1], 1 + core),
+                (got_ref.at[:, 0], 3 * (1 - core)),
+                (got_ref.at[:, 1], 2 - core),
+            )
+        ):
+            coming[c].append(
+                pltpu.make_async_copy(
+                    ref.at[:, c], v_ref.at[: DEGREE - 1, c, :, :, plane], in_sems.at[c, n]
+                )
+            )
+        mine = pl.ds(pl.multiple_of(half * core, TILE), half)
+        for n, (ref, plane) in enumerate(
+            (
+                (o_last.at[c, :, :, mine], 3 * core),
+                (n_last.at[c, :, :, mine], 1 + core),
+                (o_got.at[c], 3 * (1 - core)),
+                (n_got.at[c], 2 - core),
+            )
+        ):
+            coming[c].append(
+                pltpu.make_async_copy(
+                    ref, v_ref.at[DEGREE - 1, c, :, :, plane], in_sems.at[c, 4 + n]
+                )
+            )
+    for copies in coming:
+        for copy in copies:
+            copy.start()
     solution, residual = coefficients(gathered[:, 0, :], ct_ref)
 
     def spread(value):
@@ -599,29 +673,20 @@
         ]
 
     cs, cr = spread(solution), spread(residual)
-    own = half * core
-    copies = []
+    leaving = []
     for c in range(3):
-        for plane, refs_of, which, shift in (
-            (3 * core, os, None, own),
-            (1 + core, ns, None, own),
-            (3 * (1 - core), xs, 0, 0),
-            (2 - core, xs, 1, 0),
-        ):
+        for copy in coming[c]:
+            copy.wait()
+        for plane in range(v_ref.shape[4]):
             for t in range(half // TILE):
                 s = slice(t * TILE, (t + 1) * TILE)
                 for h in range(2):
                     z = slice(h * LANES, (h + 1) * LANES)
-                    vr, vi = src[0, c, 0, plane, s, z], src[0, c, 1, plane, s, z]
-                    sol = times((vr, vi), cs[0])
-                    res = times((vr, vi), cr[0])
+                    v = v0_ref[c, 0, plane, s, z], v0_ref[c, 1, plane, s, z]
+                    sol = times(v, cs[0])
+                    res = times(v, cr[0])
                     for k in range(1, DEGREE + 1):
-                        ref = refs_of[k - 1]
-                        if which is None:
-                            at = pl.ds(pl.multiple_of(shift + t * TILE, TILE), TILE)
-                            v = ref[c, 0, h, at, :], ref[c, 1, h, at, :]
-                        else:
-                            v = ref[which, c, 0, h, s, :], ref[which, c, 1, h, s, :]
+                        v = v_ref[k - 1, c, 0, h, plane, s, :], v_ref[k - 1, c, 1, h, plane, s, :]
                         res = plus(res, times(v, cr[k]))
                         if k < DEGREE:
                             sol = plus(sol, times(v, cs[k]))
@@ -631,8 +696,8 @@
         for n, (a, b) in enumerate(((x_ref, x_hbm), (r_ref, r_hbm))):
             copy = pltpu.make_async_copy(a.at[c], b.at[0, c], sems.at[n, c])
             copy.start()
-            copies.append(copy)
-    for copy in copies:
+            leaving.append(copy)
+    for copy in leaving:
         copy.wait()
 
 
@@ -651,13 +716,18 @@
         return pl.CostEstimate(flops=flops, bytes_accessed=0, transcendentals=0)
 
     half_x = cells_x // 2
-    away = half_x * (1 - core)
-    src_in = lax.ppermute(
-        lax.dynamic_slice_in_dim(source[0], away, half_x, axis=2), "gy", both
-    )
-    eps_in = lax.ppermute(
-        lax.dynamic_slice_in_dim(permittivity, away, half_x, axis=1), "gy", both
-    )
+    share, share_eps = (3, 2, half_x, rows, depth), (3, half_x, rows, depth)
+    moved, moved_eps, stays, stays_eps = pl.pallas_call(
+        functools.partial(split_kernel, half_x),
+        out_shape=[pltpu.VMEM(s, F32) for s in (share, share_eps) * 2],
+        in_specs=[HBM] * 2,
+        out_specs=[VMEM] * 4,
+        scratch_shapes=[pltpu.SemaphoreType.DMA((4,))],
+        compiler_params=params(62.5),
+        name="split",
+    )(source, permittivity)
+    src_in = lax.ppermute(moved, "gy", both)
+    eps_in = lax.ppermute(moved_eps, "gy", both)
     ny = 2 * rows
     field, pair = shape(3, 2, 2, ny, LANES), shape(2, 2, 2, ny, LANES)
     medium = shape(3, 2, ny, LANES)
@@ -669,52 +739,74 @@
         ],
         in_specs=[VMEM] * 5,
         out_specs=[VMEM] * 12,
-        compiler_params=params(12),
+        compiler_params=params(4),
         name="start",
-    )(source, permittivity, src_in, eps_in, frequency.reshape(1, 1))
+    )(stays, stays_eps, src_in, eps_in, frequency.reshape(1, 1))
 
     def plane(outer, k, p, q, gq, halo, m):
+        outs = [field, shape(3, 2, 2, rows, LANES)] if k + 1 == DEGREE else [field, pair, pair]
         return pl.pallas_call(
             functools.partial(plane_kernel, outer, k),
-            out_shape=[field, pair, pair],
+            out_shape=outs,
             in_specs=[VMEM] * 9,
-            out_specs=[VMEM] * 3,
-            compiler_params=params(12),
+            out_specs=[VMEM] * len(outs),
+            compiler_params=params(2),
             cost_estimate=cost(2_000_000),
             name=("outer" if outer else "inner") + str(k),
         )(p, q, gq, halo, m, cy, cz, cx, ct)
 
-    def gram(k, copies, os, ns, row):
+    halves = pltpu.HBM((DEGREE - 1, 2, 3, 2, 2, rows, LANES), F32)
+
+    def gram(k, copies, os, ns, row, held):
+        store = 0 < k < DEGREE
         outs = [shape(1, LANES) if copies == 1 else shape(copies, 1, LANES)]
-        if k:
-            outs.append(shape(2, 3, 2, 2, rows, LANES))
         args = [*os[: k + 1], *ns[: k + 1]] + ([row] if k else [])
-        got = pl.pallas_call(
+        specs = [VMEM] * len(args)
+        aliases = {}
+        if store and k > 1:
+            aliases = {len(args): 1, len(args) + 1: 2}
+            args += held
+            specs += [HBM] * 2
+        return pl.pallas_call(
             functools.partial(gram_kernel, k, copies),
-            out_shape=outs,
-            in_specs=[VMEM] * len(args),
-            out_specs=[VMEM] * len(outs),
-            compiler_params=params(12),
+            out_shape=outs + ([halves] * 2 if store else []),
+            in_specs=specs,
+            out_specs=[VMEM] + ([HBM] * 2 if store else []),
+            input_output_aliases=aliases,
+            scratch_shapes=[pltpu.SemaphoreType.DMA((2, 2))] if store else [],
+            compiler_params=params(2),
             cost_estimate=cost(500_000 * (k + 1)),
             name="gram" + str(k),
         )(*args)
-        return (got[0], lax.ppermute(got[1], "gy", both)) if k else (got[0], None)
-
-    os, ns, xs = [o], [n], []
+
+    os, ns, held = [o], [n], []
     row = None
+    far = lax.ppermute(off, ("gx", "gy"), ring)
     for k in range(DEGREE):
-        far = lax.ppermute(off, ("gx", "gy"), ring)
+        last = k + 1 == DEGREE
+        row, *held = gram(k, 1, os, ns, row, held)
+        if k:
+            on, row = lax.optimization_barrier((on, row))
         near = lax.ppermute(on, "gy", both)
-        row, x = gram(k, 1, os, ns, row)
-        if k:
-            xs.append(x)
-        o2, go2, off = plane(True, k, os[k], ns[k], gn, far, mo)
-        n2, gn2, on = plane(False, k, ns[k], os[k], go, near, mn)
-        go, gn = go2, gn2
+        o2, *edges = plane(True, k, os[k], ns[k], gn, far, mo)
+        if last:
+            own, give = held
+            lasts = edges
+            lasts[0], give, near = lax.optimization_barrier((lasts[0], give, near))
+            got = lax.ppermute(give, "gy", both)
+        else:
+            go2, off = edges
+            far = lax.ppermute(off, ("gx", "gy"), ring)
+        n2, *edges = plane(False, k, ns[k], os[k], go, near, mn)
+        if last:
+            lasts += edges
+        else:
+            gn, on = edges
+            go = go2
         os.append(o2)
         ns.append(n2)
-    row, x = gram(DEGREE, 2 * chips, os, ns, row)
-    xs.append(x)
+    lasts = [lax.ppermute(a, "gy", both) for a in lasts]
+    row = gram(DEGREE, 2 * chips, os, ns, row, None)[0]
     gathered = lax.all_to_all(row, ("gx", "gy"), split_axis=0, concat_axis=0, tiled=True)
     whole = shape(*source.shape)
     local = pltpu.VMEM(source.shape[1:], F32)
@@ -722,12 +814,20 @@
         pl.pallas_call(
             last_step_kernel,
             out_shape=[whole, whole],
-            in_specs=[VMEM] * 21,
-            out_specs=[ANY, ANY],
-            scratch_shapes=[local, local, pltpu.SemaphoreType.DMA((2, 3))],
-            compiler_params=params(16),
+            in_specs=[VMEM] * 2 + [HBM] * 3 + [ANY] * 4,
+            out_specs=[HBM, HBM],
+            scratch_shapes=[
+                local,
+                pltpu.VMEM((DEGREE, 3, 2, 2, cells_x, rows, LANES), F32),
+                local,
+                local,
+                pltpu.SemaphoreType.DMA((3,)),
+                pltpu.SemaphoreType.DMA((3, 8)),
+                pltpu.SemaphoreType.DMA((2, 3)),
+            ],
+            compiler_params=params(COMBINE_MIB),
             name="combine",
-        )(gathered, ct, source, *os[1:], *ns[1:], *xs)
+        )(gathered, ct, source, own, got, os[-1], ns[-1], *lasts)
     )
 
 

time: 97.8 us -> 87.6 us (0.90)
  blocking collectives: 0 us -> 19.3 us
  waiting for transfers between devices: 16 us -> 5.37 us
  starting transfers between devices: 50.4 us -> 41.1 us
  local copies, waits for them, and re-layouts: 7.95 us -> 0.01 us
  Pallas kernels: 21.4 us -> 20 us
    all_to_all x0 -> x1, blocking collectives: none -> 19.3 us  [body(): lax.all_to_all(row, ('gx', 'gy'), split_axis=0, concat_axis=0, tiled=True)]
    all_to_all x1 -> x0, waiting for transfers between devices: 11.6 us -> none  [body(): lax.all_to_all(row, ('gx', 'gy'), split_axis=0, concat_axis=0, tiled=True)]
    unnamed x24 -> x4, local copies, waits for them, and re-layouts: 5.91 us -> 0.01 us
    all_to_all x1 -> x0, starting transfers between devices: 5.41 us -> none  [body(): lax.all_to_all(row, ('gx', 'gy'), split_axis=0, concat_axis=0, tiled=True)]
    ppermute x6, starting transfers between devices: 32.8 us -> 28.1 us  [body(): near = lax.ppermute(on, 'gy', both)]
    dynamic_slice x2 -> x0, local copies, waits for them, and re-layouts: 2.04 us -> none  [the longest x1 1.1 us: body(): lax.dynamic_slice_in_dim(source[0], away, half_x, axis=2)]
    ppermute x6, waiting for transfers between devices: 1.26 us -> 2.82 us  [body(): near = lax.ppermute(on, 'gy', both)]
    pallas_call x19 -> x20, Pallas kernels: 15.7 us -> 14.9 us  [the longest x7 8.36 us: gram(): pl.pallas_call(functools.partial(gram_kernel, k, copies), out_shape=outs...]
  transfers between devices with their start and end apart: 21 -> 17, of which waited for: 7 -> 7; matrix products, arithmetic and copies ran while one was open for 1% -> 0% of each run, Pallas kernels for 16% -> 16%
where the time goes in v2:
time: 87.6 us; the launch traced here: 87.4 us
  starting transfers between devices  41.1 us (47%)
  Pallas kernels  20 us (23%)
  blocking collectives  19.3 us (22%)
  waiting for transfers between devices  5.37 us (6%)
  between operations  1.7 us (2%)
    ppermute x6, starting transfers between devices, body(): near = lax.ppermute(on, 'gy', both)  28.1 us
    all_to_all x1, blocking collectives, body(): lax.all_to_all(row, ('gx', 'gy'), split_axis=0, concat_axis=0, tiled=True)  19.3 us
    ppermute x1, starting transfers between devices, body(): src_in = lax.ppermute(moved, 'gy', both)  10 us
    pallas_call x7, Pallas kernels, gram(): pl.pallas_call(functools.partial(gram_kernel, k, copies), out_shape=outs...  8.36 us
    pallas_call x12, Pallas kernels, plane(): pl.pallas_call(functools.partial(plane_kernel, outer, k), out_shape=outs,...  5.29 us
    pallas_call x1, Pallas kernels, body(): pl.pallas_call(last_step_kernel, out_shape=[whole, whole], in_specs=[VMEM...  4.61 us
    ppermute x6, waiting for transfers between devices, body(): near = lax.ppermute(on, 'gy', both)  2.82 us
  transfers between devices with their start and end apart: 17, of which 7 were waited for; matrix products, arithmetic and copies ran while one was open for 0% of the time, Pallas kernels for 16%

profile of v2, /device:TPU:69, one launch (start us, length us, event | category | flops | bytes accessed | tf_op | source)
XLA Modules:
  0.0 87.4 jit_solution(2864971526652175568)
XLA Ops:
  0.6 1.3 %split.1 = (f32[3,2,2,32,256]{4,3,2,1,0:T(8,128)S(1)}, f32[3,2,32,256]{3,2,1,0:T(8,128)S(1)}, f32[3,2,2,32,256]{4,3,2,1,0:T(8,128)S(1)}, f32[3,2,32,256]{3,2,1,0:T(8,128)S(1)}) custom-call(f32[1,3,2,4,32,256]{5,4,3,2,1,0:T(8,128)} %refs_2_.1, f32[3,4,32,256]{3,2,1,0:T(8,128)} %e_hbm.1), custom_call_target="tpu_custom_call" | custom-call | tf_op jit(solution)/shard_map/split/pallas_call | solution.py:720
  1.9 10.0 %collective-permute-start = (f32[3,2,2,32,256]{4,3,2,1,0:T(8,128)S(1)}, f32[3,2,2,32,256]{4,3,2,1,0:T(8,128)S(1)}, u32[]{:S(2)}, u32[]{:S(2)}) collective-permute-start(f32[3,2,2,32,256]{4,3,2,1,0:T(8,128)S(1)} %get-tuple-element.82), channel_id=1, source_target_pairs={{0,1},{1,0},{2,3},{3,2},{4,5},{5,4},{6,7},{7,6},{8,9},{9,8},{10,11... | collective-permute-start | bytes 1179656 | tf_op jit(solution)/shard_map/ppermute | solution.py:729
  12.7 0.8 collective-permute-done.1.eps_in
  14.2 4.1 %collective-permute-start.3 = (f32[2,2,2,64,128]{4,3,2,1,0:T(8,128)S(1)}, f32[2,2,2,64,128]{4,3,2,1,0:T(8,128)S(1)}, u32[]{:S(2)}, u32[]{:S(2)}) collective-permute-start(f32[2,2,2,64,128]{4,3,2,1,0:T(8,128)S(1)} %get-tuple-element.95), channel_id=1, source_target_pairs={{0,1},{1,0},{2,3},{3,2},{4,5},{5,4},{6,7},{7,6},{8,9},{9,8},{10,11... | collective-permute-start | bytes 786440 | tf_op jit(solution)/shard_map/ppermute | solution.py:790
  18.5 1.7 %collective-permute-done.2.refs_3_ = f32[2,2,2,64,128]{4,3,2,1,0:T(8,128)S(1)} collective-permute-done((f32[2,2,2,64,128]{4,3,2,1,0:T(8,128)S(1)}, f32[2,2,2,64,128]{4,3,2,1,0:T(8,128)S(1)}, u32[]{:S(2)}, u32[]{:S(2)}) %collective-permute-start.2) | collective-permute-done | bytes 262176 | tf_op jit(solution)/shard_map/ppermute | solution.py:784
  20.2 0.5 outer0.1
  20.8 0.5 inner0.1
  21.3 1.1 %gram1.1 = (f32[1,128]{1,0:T(1,128)S(1)}, f32[5,2,3,2,2,32,128]{6,5,4,3,2,1,0:T(8,128)}, f32[5,2,3,2,2,32,128]{6,5,4,3,2,1,0:T(8,128)}) custom-call(f32[3,2,2,64,128]{4,3,2,1,0:T(8,128)S(1)} %get-tuple-element.84.refs_0_.refs_1_, f32[3,2,2,64,128]{4,3,2,1,0:T(8,128)S(1)} %get-tuple-element.93.refs_0_.refs_1_, ...), custom_call_target="tpu_custom_call" | custom-call | flops 1000000 | tf_op jit(solution)/shard_map/gram1/pallas_call | solution.py:770
  22.5 5.1 %collective-permute-start.5 = (f32[2,2,2,64,128]{4,3,2,1,0:T(8,128)S(1)}, f32[2,2,2,64,128]{4,3,2,1,0:T(8,128)S(1)}, u32[]{:S(2)}, u32[]{:S(2)}) collective-permute-start(f32[2,2,2,64,128]{4,3,2,1,0:T(8,128)S(1)} %get-tuple-element.104), channel_id=1, source_target_pairs={{0,1},{1,0},{2,3},{3,2},{4,5},{5,4},{6,7},{7,6},{8,9},{9,8},{10,11... | collective-permute-start | bytes 786440 | tf_op jit(solution)/shard_map/ppermute | solution.py:790
  27.6 0.5 outer1.1
  28.2 0.6 collective-permute-done.5.refs_3_
  28.8 0.5 inner1.1
  29.2 1.2 %gram2.1 = (f32[1,128]{1,0:T(1,128)S(1)}, f32[5,2,3,2,2,32,128]{6,5,4,3,2,1,0:T(8,128)}, f32[5,2,3,2,2,32,128]{6,5,4,3,2,1,0:T(8,128)}) custom-call(f32[3,2,2,64,128]{4,3,2,1,0:T(8,128)S(1)} %get-tuple-element.84.refs_0_.refs_1_, f32[3,2,2,64,128]{4,3,2,1,0:T(8,128)S(1)} %get-tuple-element.93.refs_0_.refs_1_, ...), custom_call_target="tpu_custom_call", output_to_operand_aliasing={{1}: (7, {}), {2}: (8, {})} | custom-call | flops 1500000 | tf_op jit(solution)/shard_map/gram2/pallas_call | solution.py:770
  30.5 4.8 %collective-permute-start.7 = (f32[2,2,2,64,128]{4,3,2,1,0:T(8,128)S(1)}, f32[2,2,2,64,128]{4,3,2,1,0:T(8,128)S(1)}, u32[]{:S(2)}, u32[]{:S(2)}) collective-permute-start(f32[2,2,2,64,128]{4,3,2,1,0:T(8,128)S(1)} %get-tuple-element.115), channel_id=1, source_target_pairs={{0,1},{1,0},{2,3},{3,2},{4,5},{5,4},{6,7},{7,6},{8,9},{9,8},{10,11... | collective-permute-start | bytes 786440 | tf_op jit(solution)/shard_map/ppermute | solution.py:790
  35.3 0.5 outer2.1
  35.9 0.6 collective-permute-done.7.refs_3_
  36.9 1.3 %gram3.1 = (f32[1,128]{1,0:T(1,128)S(1)}, f32[5,2,3,2,2,32,128]{6,5,4,3,2,1,0:T(8,128)}, f32[5,2,3,2,2,32,128]{6,5,4,3,2,1,0:T(8,128)}) custom-call(f32[3,2,2,64,128]{4,3,2,1,0:T(8,128)S(1)} %get-tuple-element.84.refs_0_.refs_1_, f32[3,2,2,64,128]{4,3,2,1,0:T(8,128)S(1)} %get-tuple-element.93.refs_0_.refs_1_, ...), custom_call_target="tpu_custom_call", output_to_operand_aliasing={{1}: (9, {}), {2}: (10, {})} | custom-call | flops 2000000 | tf_op jit(solution)/shard_map/gram3/pallas_call | solution.py:770
  38.2 4.7 %collective-permute-start.9 = (f32[2,2,2,64,128]{4,3,2,1,0:T(8,128)S(1)}, f32[2,2,2,64,128]{4,3,2,1,0:T(8,128)S(1)}, u32[]{:S(2)}, u32[]{:S(2)}) collective-permute-start(f32[2,2,2,64,128]{4,3,2,1,0:T(8,128)S(1)} %get-tuple-element.126), channel_id=1, source_target_pairs={{0,1},{1,0},{2,3},{3,2},{4,5},{5,4},{6,7},{7,6},{8,9},{9,8},{10,11... | collective-permute-start | bytes 786440 | tf_op jit(solution)/shard_map/ppermute | solution.py:790
  42.9 0.5 outer3.1
  44.1 0.5 inner3.1
  44.6 1.5 %gram4.1 = (f32[1,128]{1,0:T(1,128)S(1)}, f32[5,2,3,2,2,32,128]{6,5,4,3,2,1,0:T(8,128)}, f32[5,2,3,2,2,32,128]{6,5,4,3,2,1,0:T(8,128)}) custom-call(f32[3,2,2,64,128]{4,3,2,1,0:T(8,128)S(1)} %get-tuple-element.84.refs_0_.refs_1_, f32[3,2,2,64,128]{4,3,2,1,0:T(8,128)S(1)} %get-tuple-element.93.refs_0_.refs_1_, ...), custom_call_target="tpu_custom_call", output_to_operand_aliasing={{1}: (11, {}), {2}: (12, {})} | custom-call | flops 2500000 | tf_op jit(solution)/shard_map/gram4/pallas_call | solution.py:770
  46.1 4.8 %collective-permute-start.11 = (f32[2,2,2,64,128]{4,3,2,1,0:T(8,128)S(1)}, f32[2,2,2,64,128]{4,3,2,1,0:T(8,128)S(1)}, u32[]{:S(2)}, u32[]{:S(2)}) collective-permute-start(f32[2,2,2,64,128]{4,3,2,1,0:T(8,128)S(1)} %get-tuple-element.137), channel_id=1, source_target_pairs={{0,1},{1,0},{2,3},{3,2},{4,5},{5,4},{6,7},{7,6},{8,9},{9,8},{10,11... | collective-permute-start | bytes 786440 | tf_op jit(solution)/shard_map/ppermute | solution.py:790
  50.9 0.5 outer4.1
  51.5 0.6 collective-permute-done.11.refs_3_
  52.5 1.6 %gram5.1 = (f32[1,128]{1,0:T(1,128)S(1)}, f32[5,2,3,2,2,32,128]{6,5,4,3,2,1,0:T(8,128)}, f32[5,2,3,2,2,32,128]{6,5,4,3,2,1,0:T(8,128)}) custom-call(f32[3,2,2,64,128]{4,3,2,1,0:T(8,128)S(1)} %get-tuple-element.84.refs_0_.refs_1_, f32[3,2,2,64,128]{4,3,2,1,0:T(8,128)S(1)} %get-tuple-element.93.refs_0_.refs_1_, ...), custom_call_target="tpu_custom_call", output_to_operand_aliasing={{1}: (13, {}), {2}: (14, {})} | custom-call | flops 3000000 | tf_op jit(solution)/shard_map/gram5/pallas_call | solution.py:770
  54.1 4.5 %collective-permute-start.13 = (f32[2,2,2,64,128]{4,3,2,1,0:T(8,128)S(1)}, f32[2,2,2,64,128]{4,3,2,1,0:T(8,128)S(1)}, u32[]{:S(2)}, u32[]{:S(2)}) collective-permute-start(f32[2,2,2,64,128]{4,3,2,1,0:T(8,128)S(1)} %get-tuple-element.150), channel_id=1, source_target_pairs={{0,1},{1,0},{2,3},{3,2},{4,5},{5,4},{6,7},{7,6},{8,9},{9,8},{10,11... | collective-permute-start | bytes 786440 | tf_op jit(solution)/shard_map/ppermute | solution.py:790
  59.0 0.8 collective-permute-done.13.refs_3_
  59.7 1.2 %collective-permute-start.14 = (f32[5,2,3,2,2,32,128]{6,5,4,3,2,1,0:T(8,128)}, f32[5,2,3,2,2,32,128]{6,5,4,3,2,1,0:T(8,128)S(1)}, u32[]{:S(2)}, u32[]{:S(2)}) collective-permute-start(f32[5,2,3,2,2,32,128]{6,5,4,3,2,1,0:T(8,128)} %get-tuple-element.155), channel_id=1, source_target_pairs={{0,1},{1,0},{2,3},{3,2},{4,5},{5,4},{6,7},{7,6},{8,9},{9,8},{10,11... | collective-permute-start | bytes 5898248 | tf_op jit(solution)/shard_map/ppermute | solution.py:796
  61.5 0.5 collective-permute-start.16
  62.0 1.3 %gram6.1 = f32[32,1,128]{2,1,0:T(1,128)S(1)} custom-call(f32[3,2,2,64,128]{4,3,2,1,0:T(8,128)S(1)} %get-tuple-element.84.refs_0_.refs_1_, f32[3,2,2,64,128]{4,3,2,1,0:T(8,128)S(1)} %get-tuple-element.93.refs_0_.refs_1_, f32[3,2,2,64,128]{4,3,2,1,0:T(8,128)S(1)} %get-tuple-element.100.refs_0_.refs_2_.refs_1_, ...), custom_call_target="tpu_custom_call" | custom-call | flops 3500000 | tf_op jit(solution)/shard_map/gram6/pallas_call | solution.py:770
  63.3 19.3 %all_to_all.5.refs_0_ = f32[32,1,128]{2,1,0:T(1,128)S(1)} all-to-all(f32[32,1,128]{2,1,0:T(1,128)S(1)} %gram6.1), channel_id=1, replica_groups=mesh['groups'=4,'gx'=16,'gy'=2] {'gx','gy'}, dimensions={0} | all-to-all | bytes 32768 | tf_op jit(solution)/shard_map/all_to_all | solution.py:810
  82.6 4.6 %combine.1 = (f32[1,3,2,4,32,256]{5,4,3,2,1,0:T(8,128)}, f32[1,3,2,4,32,256]{5,4,3,2,1,0:T(8,128)}) custom-call(f32[32,1,128]{2,1,0:T(1,128)S(1)} %all_to_all.5.refs_0_, f32[8,128]{1,0:T(8,128)S(1)} %get-tuple-element.92.refs_8_.refs_1_, f32[1,3,2,4,32,256]{5,4,3,2,1,0:T(8,128)S(1)} %copy-done.1, f32[5,2,3,2,2,32,128]{6,5,4,3,2,1,0:T(8,128)S(1)} %copy-done, ...), custom_call_target="tpu_custom_call" | custom-call | tf_op jit(solution)/shard_map/combine/pallas_call | solution.py:814
  (29 shorter events, 4.0 us)
Async XLA Ops:
  1.9 11.7 %collective-permute-start = (f32[3,2,2,32,256]{4,3,2,1,0:T(8,128)S(1)}, f32[3,2,2,32,256]{4,3,2,1,0:T(8,128)S(1)}, u32[]{:S(2)}, u32[]{:S(2)}) collective-permute-start(f32[3,2,2,32,256]{4,3,2,1,0:T(8,128)S(1)} %get-tuple-element.82), channel_id=1, source_target_pairs={{0,1},{1,0},{2,3},{3,2},{4,5},{5,4},{6,7},{7,6},{8,9},{9,8},{10,11... | collective-permute-start | bytes 1179656 | tf_op jit(solution)/shard_map/ppermute | solution.py:729
  12.0 1.6 %collective-permute-start.1 = (f32[3,2,32,256]{3,2,1,0:T(8,128)S(1)}, f32[3,2,32,256]{3,2,1,0:T(8,128)S(1)}, u32[]{:S(2)}, u32[]{:S(2)}) collective-permute-start(f32[3,2,32,256]{3,2,1,0:T(8,128)S(1)} %get-tuple-element.83), channel_id=1, source_target_pairs={{0,1},{1,0},{2,3},{3,2},{4,5},{5,4},{6,7},{7,6},{8,9},{9,8},{10,11... | collective-permute-start | bytes 589832 | tf_op jit(solution)/shard_map/ppermute | solution.py:730
  14.0 6.2 %collective-permute-start.2 = (f32[2,2,2,64,128]{4,3,2,1,0:T(8,128)S(1)}, f32[2,2,2,64,128]{4,3,2,1,0:T(8,128)S(1)}, u32[]{:S(2)}, u32[]{:S(2)}) collective-permute-start(f32[2,2,2,64,128]{4,3,2,1,0:T(8,128)S(1)} %get-tuple-element.87), channel_id=1, source_target_pairs={{1,2},{3,4},{5,6},{7,8},{9,10},{11,12},{13,14},{15,16},{17,18},{19... | collective-permute-start | bytes 786440 | tf_op jit(solution)/shard_map/ppermute | solution.py:784
  14.2 6.7 %collective-permute-start.3 = (f32[2,2,2,64,128]{4,3,2,1,0:T(8,128)S(1)}, f32[2,2,2,64,128]{4,3,2,1,0:T(8,128)S(1)}, u32[]{:S(2)}, u32[]{:S(2)}) collective-permute-start(f32[2,2,2,64,128]{4,3,2,1,0:T(8,128)S(1)} %get-tuple-element.95), channel_id=1, source_target_pairs={{0,1},{1,0},{2,3},{3,2},{4,5},{5,4},{6,7},{7,6},{8,9},{9,8},{10,11... | collective-permute-start | bytes 786440 | tf_op jit(solution)/shard_map/ppermute | solution.py:790
  20.7 6.9 %collective-permute-start.4 = (f32[2,2,2,64,128]{4,3,2,1,0:T(8,128)S(1)}, f32[2,2,2,64,128]{4,3,2,1,0:T(8,128)S(1)}, u32[]{:S(2)}, u32[]{:S(2)}) collective-permute-start(f32[2,2,2,64,128]{4,3,2,1,0:T(8,128)S(1)} %get-tuple-element.99), channel_id=1, source_target_pairs={{1,2},{3,4},{5,6},{7,8},{9,10},{11,12},{13,14},{15,16},{17,18},{19... | collective-permute-start | bytes 786440 | tf_op jit(solution)/shard_map/ppermute | solution.py:799
  22.5 6.3 %collective-permute-start.5 = (f32[2,2,2,64,128]{4,3,2,1,0:T(8,128)S(1)}, f32[2,2,2,64,128]{4,3,2,1,0:T(8,128)S(1)}, u32[]{:S(2)}, u32[]{:S(2)}) collective-permute-start(f32[2,2,2,64,128]{4,3,2,1,0:T(8,128)S(1)} %get-tuple-element.104), channel_id=1, source_target_pairs={{0,1},{1,0},{2,3},{3,2},{4,5},{5,4},{6,7},{7,6},{8,9},{9,8},{10,11... | collective-permute-start | bytes 786440 | tf_op jit(solution)/shard_map/ppermute | solution.py:790
  28.1 7.2 %collective-permute-start.6 = (f32[2,2,2,64,128]{4,3,2,1,0:T(8,128)S(1)}, f32[2,2,2,64,128]{4,3,2,1,0:T(8,128)S(1)}, u32[]{:S(2)}, u32[]{:S(2)}) collective-permute-start(f32[2,2,2,64,128]{4,3,2,1,0:T(8,128)S(1)} %get-tuple-element.107), channel_id=1, source_target_pairs={{1,2},{3,4},{5,6},{7,8},{9,10},{11,12},{13,14},{15,16},{17,18},{19... | collective-permute-start | bytes 786440 | tf_op jit(solution)/shard_map/ppermute | solution.py:799
  30.5 6.0 %collective-permute-start.7 = (f32[2,2,2,64,128]{4,3,2,1,0:T(8,128)S(1)}, f32[2,2,2,64,128]{4,3,2,1,0:T(8,128)S(1)}, u32[]{:S(2)}, u32[]{:S(2)}) collective-permute-start(f32[2,2,2,64,128]{4,3,2,1,0:T(8,128)S(1)} %get-tuple-element.115), channel_id=1, source_target_pairs={{0,1},{1,0},{2,3},{3,2},{4,5},{5,4},{6,7},{7,6},{8,9},{9,8},{10,11... | collective-permute-start | bytes 786440 | tf_op jit(solution)/shard_map/ppermute | solution.py:790
  35.7 7.2 %collective-permute-start.8 = (f32[2,2,2,64,128]{4,3,2,1,0:T(8,128)S(1)}, f32[2,2,2,64,128]{4,3,2,1,0:T(8,128)S(1)}, u32[]{:S(2)}, u32[]{:S(2)}) collective-permute-start(f32[2,2,2,64,128]{4,3,2,1,0:T(8,128)S(1)} %get-tuple-element.118), channel_id=1, source_target_pairs={{1,2},{3,4},{5,6},{7,8},{9,10},{11,12},{13,14},{15,16},{17,18},{19... | collective-permute-start | bytes 786440 | tf_op jit(solution)/shard_map/ppermute | solution.py:799
  38.2 5.9 %collective-permute-start.9 = (f32[2,2,2,64,128]{4,3,2,1,0:T(8,128)S(1)}, f32[2,2,2,64,128]{4,3,2,1,0:T(8,128)S(1)}, u32[]{:S(2)}, u32[]{:S(2)}) collective-permute-start(f32[2,2,2,64,128]{4,3,2,1,0:T(8,128)S(1)} %get-tuple-element.126), channel_id=1, source_target_pairs={{0,1},{1,0},{2,3},{3,2},{4,5},{5,4},{6,7},{7,6},{8,9},{9,8},{10,11... | collective-permute-start | bytes 786440 | tf_op jit(solution)/shard_map/ppermute | solution.py:790
  43.4 7.5 %collective-permute-start.10 = (f32[2,2,2,64,128]{4,3,2,1,0:T(8,128)S(1)}, f32[2,2,2,64,128]{4,3,2,1,0:T(8,128)S(1)}, u32[]{:S(2)}, u32[]{:S(2)}) collective-permute-start(f32[2,2,2,64,128]{4,3,2,1,0:T(8,128)S(1)} %get-tuple-element.129), channel_id=1, source_target_pairs={{1,2},{3,4},{5,6},{7,8},{9,10},{11,12},{13,14},{15,16},{17,18},{19... | collective-permute-start | bytes 786440 | tf_op jit(solution)/shard_map/ppermute | solution.py:799
  46.1 6.0 %collective-permute-start.11 = (f32[2,2,2,64,128]{4,3,2,1,0:T(8,128)S(1)}, f32[2,2,2,64,128]{4,3,2,1,0:T(8,128)S(1)}, u32[]{:S(2)}, u32[]{:S(2)}) collective-permute-start(f32[2,2,2,64,128]{4,3,2,1,0:T(8,128)S(1)} %get-tuple-element.137), channel_id=1, source_target_pairs={{0,1},{1,0},{2,3},{3,2},{4,5},{5,4},{6,7},{7,6},{8,9},{9,8},{10,11... | collective-permute-start | bytes 786440 | tf_op jit(solution)/shard_map/ppermute | solution.py:790
  51.3 7.3 %collective-permute-start.12 = (f32[2,2,2,64,128]{4,3,2,1,0:T(8,128)S(1)}, f32[2,2,2,64,128]{4,3,2,1,0:T(8,128)S(1)}, u32[]{:S(2)}, u32[]{:S(2)}) collective-permute-start(f32[2,2,2,64,128]{4,3,2,1,0:T(8,128)S(1)} %get-tuple-element.140), channel_id=1, source_target_pairs={{1,2},{3,4},{5,6},{7,8},{9,10},{11,12},{13,14},{15,16},{17,18},{19... | collective-permute-start | bytes 786440 | tf_op jit(solution)/shard_map/ppermute | solution.py:799
  54.1 5.6 %collective-permute-start.13 = (f32[2,2,2,64,128]{4,3,2,1,0:T(8,128)S(1)}, f32[2,2,2,64,128]{4,3,2,1,0:T(8,128)S(1)}, u32[]{:S(2)}, u32[]{:S(2)}) collective-permute-start(f32[2,2,2,64,128]{4,3,2,1,0:T(8,128)S(1)} %get-tuple-element.150), channel_id=1, source_target_pairs={{0,1},{1,0},{2,3},{3,2},{4,5},{5,4},{6,7},{7,6},{8,9},{9,8},{10,11... | collective-permute-start | bytes 786440 | tf_op jit(solution)/shard_map/ppermute | solution.py:790
  59.7 22.9 %collective-permute-start.14 = (f32[5,2,3,2,2,32,128]{6,5,4,3,2,1,0:T(8,128)}, f32[5,2,3,2,2,32,128]{6,5,4,3,2,1,0:T(8,128)S(1)}, u32[]{:S(2)}, u32[]{:S(2)}) collective-permute-start(f32[5,2,3,2,2,32,128]{6,5,4,3,2,1,0:T(8,128)} %get-tuple-element.155), channel_id=1, source_target_pairs={{0,1},{1,0},{2,3},{3,2},{4,5},{5,4},{6,7},{7,6},{8,9},{9,8},{10,11... | collective-permute-start | bytes 5898248 | tf_op jit(solution)/shard_map/ppermute | solution.py:796
  61.0 21.6 %collective-permute-start.15 = (f32[3,2,2,32,128]{4,3,2,1,0:T(8,128)S(1)}, f32[3,2,2,32,128]{4,3,2,1,0:T(8,128)S(1)}, u32[]{:S(2)}, u32[]{:S(2)}) collective-permute-start(f32[3,2,2,32,128]{4,3,2,1,0:T(8,128)S(1)} %get-tuple-element.156), channel_id=1, source_target_pairs={{0,1},{1,0},{2,3},{3,2},{4,5},{5,4},{6,7},{7,6},{8,9},{9,8},{10,11... | collective-permute-start | bytes 589832 | tf_op jit(solution)/shard_map/ppermute | solution.py:808
  61.5 21.1 %collective-permute-start.16 = (f32[3,2,2,32,128]{4,3,2,1,0:T(8,128)S(1)}, f32[3,2,2,32,128]{4,3,2,1,0:T(8,128)S(1)}, u32[]{:S(2)}, u32[]{:S(2)}) collective-permute-start(f32[3,2,2,32,128]{4,3,2,1,0:T(8,128)S(1)} %get-tuple-element.157), channel_id=1, source_target_pairs={{0,1},{1,0},{2,3},{3,2},{4,5},{5,4},{6,7},{7,6},{8,9},{9,8},{10,11... | collective-permute-start | bytes 589832 | tf_op jit(solution)/shard_map/ppermute | solution.py:808
  62.0 20.6 %copy-start = (f32[5,2,3,2,2,32,128]{6,5,4,3,2,1,0:T(8,128)S(1)}, f32[5,2,3,2,2,32,128]{6,5,4,3,2,1,0:T(8,128)}, u32[]{:S(2)}) copy-start(f32[5,2,3,2,2,32,128]{6,5,4,3,2,1,0:T(8,128)} %get-tuple-element.154.refs_3_) | copy-start | bytes 5898244
  62.0 20.7 %copy-start.1 = (f32[1,3,2,4,32,256]{5,4,3,2,1,0:T(8,128)S(1)}, f32[1,3,2,4,32,256]{5,4,3,2,1,0:T(8,128)}, u32[]{:S(2)}) copy-start(f32[1,3,2,4,32,256]{5,4,3,2,1,0:T(8,128)} %refs_2_.1) | copy-start | bytes 2359300
